TPU v7x, 32 devices: a 4x4x1 block of a 4x4x8 slice. The times are simulated.
32 devices in a mesh: dp: 1 (over z), ffn: 4 (over y), emb: 8 (over x, core).
Axes of the slice: x: 4, y: 4, z: 1, core: 2. Of those that a mesh axis runs over, the one named last changes fastest.
The devices are a block of a 4x4x8 slice.
Arguments:
- hidden: bfloat16 [2048, 2048], P('dp', 'emb')
- norm_pre: bfloat16 [2048], P('emb')
- norm_post: bfloat16 [2048], P('emb')
- w_router: bfloat16 [2048, 64], P('emb')
- w_gate: bfloat16 [64, 2048, 1024], P(None, 'emb', 'ffn')
- w_up: bfloat16 [64, 2048, 1024], P(None, 'emb', 'ffn')
- w_down: bfloat16 [64, 1024, 2048], P(None, 'ffn', 'emb')
- choice: int32 [2048, 8], P('dp')
Outputs:
- output: bfloat16 [2048, 2048], P('dp', 'emb')
All inputs are finite; a program needn't handle non-finite values.
Results may differ from a plain program's by a relative error of at most 0.0143155.
Values are sent between devices in bfloat16 or wider.
A program may use at most 768 MiB of HBM per device.

v0:
```python
import jax
import jax.numpy as jnp
from jax import lax
from jax.sharding import PartitionSpec as P

EPS = 1e-5


def route_tokens(choice, router_prob, experts, capacity):
    num_tok, top_k = choice.shape
    onehot = (choice[:, :, None] == jnp.arange(experts)[None, None, :]).astype(jnp.int32)
    assigned = jnp.sum(onehot, axis=1)
    before = jnp.cumsum(assigned, axis=0) - assigned
    slot_idx = jnp.sum(onehot * before[:, None, :], axis=2)
    position = jnp.where(slot_idx < capacity, choice * capacity + slot_idx, experts * capacity)
    gate_val = jnp.take_along_axis(router_prob, choice, axis=1)
    flat_pos = position.reshape(-1)
    token_ids = jnp.repeat(jnp.arange(num_tok, dtype=jnp.int32), top_k)
    slot_token = jnp.full((experts * capacity,), num_tok, jnp.int32).at[flat_pos].set(token_ids, mode='drop')
    slot_gate = jnp.zeros((experts * capacity,), jnp.float32).at[flat_pos].set(gate_val.reshape(-1), mode='drop')
    return position, slot_token, slot_gate


def solution(mesh):
    emb_size = mesh.shape['emb']

    def local_block(hidden, norm_pre, norm_post, w_router, w_gate, w_up, w_down, choice):
        num_tok, local_width = hidden.shape
        model_width = local_width * emb_size
        experts = w_gate.shape[0]
        top_k = choice.shape[1]
        capacity = 2 * num_tok * top_k // experts
        hid_f32 = hidden.astype(jnp.float32)
        sq_pre = lax.psum(jnp.sum(hid_f32 * hid_f32, axis=1, keepdims=True), 'emb')
        inv_pre = lax.rsqrt(sq_pre / model_width + EPS)
        normed = (hid_f32 * inv_pre * norm_pre.astype(jnp.float32)).astype(jnp.bfloat16)
        logits = lax.psum(jnp.dot(normed, w_router, preferred_element_type=jnp.float32), 'emb')
        router_prob = jax.nn.softmax(logits, axis=1)
        position, slot_token, slot_gate = route_tokens(choice, router_prob, experts, capacity)
        expert_in = jnp.take(normed, slot_token, axis=0, mode='fill', fill_value=0).reshape(experts, capacity, local_width)
        z_gate = jnp.einsum('ecd,edf->ecf', expert_in, w_gate, preferred_element_type=jnp.float32).astype(jnp.bfloat16)
        z_up = jnp.einsum('ecd,edf->ecf', expert_in, w_up, preferred_element_type=jnp.float32).astype(jnp.bfloat16)
        z_gate, z_up = lax.psum((z_gate, z_up), 'emb')
        act_val = (jax.nn.gelu(z_gate.astype(jnp.float32), approximate=True) * z_up.astype(jnp.float32)).astype(jnp.bfloat16)
        part_out = jnp.einsum('ecf,efd->ecd', act_val, w_down, preferred_element_type=jnp.float32).astype(jnp.bfloat16)
        expert_out = lax.psum(part_out, 'ffn')
        weighted = (expert_out.reshape(experts * capacity, local_width).astype(jnp.float32) * slot_gate[:, None]).astype(jnp.bfloat16)
        picked = jnp.take(weighted, position, axis=0, mode='fill', fill_value=0)
        mix_sum = jnp.sum(picked.astype(jnp.float32), axis=1)
        sq_post = lax.psum(jnp.sum(mix_sum * mix_sum, axis=1, keepdims=True), 'emb')
        inv_post = lax.rsqrt(sq_post / model_width + EPS)
        return (hid_f32 + mix_sum * inv_post * norm_post.astype(jnp.float32)).astype(jnp.bfloat16)

    in_specs = (P('dp', 'emb'), P('emb'), P('emb'), P('emb', None), P(None, 'emb', 'ffn'), P(None, 'emb', 'ffn'), P(None, 'ffn', 'emb'), P('dp', None))
    return jax.shard_map(local_block, mesh=mesh, in_specs=in_specs, out_specs=P('dp', 'emb'), check_vma=False)
```

profile of v0, /device:TPU:97, one launch (start us, length us, event | category | flops | bytes accessed | tf_op | source)
XLA Modules:
  0.0 1083.3 jit_solution(2448471380931338791)
XLA Ops:
  6.6 1.5 convert_reduce_fusion.1
  8.1 18.1 %reduce-window.6 = s32[64,16,128]{2,1,0:T(8,128)S(1)} reduce-window(s32[64,16,128]{2,1,0:T(8,128)S(1)} %bitcast.42, s32[]{:T(128)} %constant.30.clone.1), window={size=1x1x128 pad=0_0x0_0x127_0}, to_apply=%region_1.0 | reduce-window | flops 16646144 | bytes 1048580 | tf_op jit(solution)/shard_map/reduce-window
  27.5 1.5 select_reduce_fusion
  29.1 0.9 compare_and_fusion.1
  30.3 0.5 reshape.87
  31.5 60.4 %scatter_custom_fusion = s32[32768]{0:T(1024)S(1)} fusion(s32[16384]{0:T(1024)S(1)} %bitcast.45, s32[16384]{0:T(1024)S(1)} %reshape.116, s32[]{:T(128)} %constant.34.clone.1), kind=kCustom, calls=%fused_computation.54 | custom fusion | bytes 131076 | tf_op jit(solution)/shard_map/scatter | solution.py:19
  92.3 14.1 %psum.42 = f32[2048,1]{0,1:T(1,128)S(1)} all-reduce(f32[2048,1]{0,1:T(1,128)S(1)} %bitcast.49), channel_id=1, replica_groups=mesh['dp'=1,'ffn'=4,'emb'=8] {'emb'}, use_global_device_ids=true, to_apply=%region_6.0 | all-reduce | flops 2048 | bytes 16384 | tf_op jit(solution)/shard_map/psum | solution.py:34
  106.8 128.6 %gather_fusion = bf16[32768,256]{1,0:T(8,128)(2,1)} fusion(bf16[2048,256]{1,0:T(8,128)(2,1)S(1)} %fusion.20, s32[32768]{0:T(1024)S(1)} %fusion.25), kind=kCustom, calls=%fused_computation | custom fusion | bytes 33685504 | tf_op jit(solution)/shard_map/jit(_take)/gather | solution.py:40
  235.4 18.0 %fusion.15 = bf16[64,512,256]{2,1,0:T(8,128)(2,1)} fusion(bf16[64,256,256]{2,1,0:T(8,128)(2,1)} %param.13, bf16[64,512,256]{2,1,0:T(8,128)(2,1)} %bitcast.38, pred[64,512]{1,0:T(8,128)(4,1)S(1)} %broadcast_in_dim.63), kind=kOutput, calls=%fused_computation.24 | convolution fusion | flops 4311744512 | bytes 41975808 | tf_op jit(solution)/shard_map/ecd,edf->ecf/dot_general | solution.py:42
  253.4 1.2 copy-done.3
  254.6 12.8 %fusion.14 = bf16[64,512,256]{2,1,0:T(8,128)(2,1)} fusion(bf16[64,256,256]{2,1,0:T(8,128)(2,1)} %param.12, bf16[64,512,256]{2,1,0:T(8,128)(2,1)S(1)} %bitcast.39, pred[64,512]{1,0:T(8,128)(4,1)S(1)} %broadcast_in_dim.63), kind=kOutput, calls=%fused_computation.23 | convolution fusion | flops 4311744512 | bytes 41975808 | tf_op jit(solution)/shard_map/ecd,edf->ecf/dot_general | solution.py:41
  267.6 1.2 fusion.36
  269.1 335.7 %all-reduce.9.cloned.1.call-done = (bf16[64,512,256]{2,1,0:T(8,128)(2,1)}, bf16[64,512,256]{2,1,0:T(8,128)(2,1)}) async-done(((bf16[64,512,256]{2,1,0:T(8,128)(2,1)}, bf16[64,512,256]{2,1,0:T(8,128)(2,1)}), (bf16[64,512,256]{2,1,0:T(8,128)(2,1)}, bf16[64,512,256]{2,1,0:T(8,128)(2,1)})) %all-reduce.9.cloned.1.call-update) | async-done | bytes 33554448 | tf_op jit(solution)/shard_map/psum | solution.py:43
  604.8 25.4 %fusion.11 = bf16[64,512,256]{2,1,0:T(8,128)(2,1)} fusion(bf16[64,256,256]{2,1,0:T(8,128)(2,1)} %param.14, bf16[64,512,256]{2,1,0:T(8,128)(2,1)} %get-tuple-element.5, bf16[64,512,256]{2,1,0:T(8,128)(2,1)} %get-tuple-element.6), kind=kOutput, calls=%fused_computation.22 | convolution fusion | flops 4404019200 | bytes 58720256 | tf_op jit(solution)/shard_map/ecf,efd->ecd/dot_general | solution.py:45
  630.3 0.6 copy-done.12
  630.9 0.5 convert_element_type.62
  631.5 1.0 copy.25
  633.7 0.5 reshape.106
  634.2 0.6 broadcast_clamp_fusion
  634.9 26.1 %all-reduce.7.cloned.1.call-done = f32[2048,64]{0,1:T(8,128)} async-done(((f32[2048,64]{0,1:T(8,128)}), f32[2048,64]{0,1:T(8,128)}) %all-reduce.7.cloned.1.call-update) | async-done | bytes 524304 | tf_op jit(solution)/shard_map/psum | solution.py:37
  661.0 1.1 reduce_max.9
  662.1 1.1 fusion.24
  663.2 1.1 fusion.23
  664.4 130.6 %gather_fusion.2 = f32[16384]{0:T(1024)S(1)} fusion(f32[2048,64]{0,1:T(8,128)S(1)} %fusion.23, s32[16384]{0:T(1024)S(1)} %reshape.106), kind=kCustom, calls=%fused_computation.2 | custom fusion | bytes 262144 | tf_op jit(solution)/shard_map/jit(take_along_axis)/gather | solution.py:16
  794.9 0.6 reshape.109
  796.7 60.8 %scatter_custom_fusion.1 = f32[32768]{0:T(1024)S(1)} fusion(s32[16384]{0:T(1024)} %bitcast.46, f32[16384]{0:T(1024)S(1)} %reshape.124, f32[]{:T(128)} %constant.42.clone.1), kind=kCustom, calls=%fused_computation.52 | custom fusion | bytes 131584 | tf_op jit(solution)/shard_map/scatter | solution.py:20
  857.5 97.3 %all-reduce.5.cloned.1.call-done = bf16[32768,256]{1,0:T(8,128)(2,1)} async-done(((bf16[32768,256]{1,0:T(8,128)(2,1)}), bf16[32768,256]{1,0:T(8,128)(2,1)}) %all-reduce.5.cloned.1.call-update) | async-done | bytes 16777232 | tf_op jit(solution)/shard_map/psum | solution.py:46
  954.7 15.3 %multiply_convert_fusion = bf16[32768,256]{1,0:T(8,128)(2,1)} fusion(bf16[32768,256]{1,0:T(8,128)(2,1)} %all-reduce.5.cloned.1.call-done, f32[32768]{0:T(1024)S(1)} %scatter_custom_fusion.1), kind=kLoop, calls=%fused_computation.16 | loop fusion | flops 25165824 | bytes 33685504 | tf_op jit(solution)/shard_map/convert_element_type | solution.py:47
  970.1 68.8 %gather_fusion.1 = bf16[16384,256]{1,0:T(8,128)(2,1)} fusion(bf16[32768,256]{1,0:T(8,128)(2,1)} %multiply_convert_fusion, s32[16384]{0:T(1024)S(1)} %copy-done.2), kind=kCustom, calls=%fused_computation.1 | custom fusion | bytes 16842752 | tf_op jit(solution)/shard_map/jit(_take)/gather | solution.py:48
  1038.9 23.1 %convert_reduce_fusion = f32[2048,256]{1,0:T(8,128)S(1)} fusion(bf16[16384,256]{1,0:T(8,128)(2,1)} %gather_fusion.1, pred[2048,8]{1,0:T(8,128)(4,1)S(1)} %copy-done.8), kind=kLoop, calls=%fused_computation.17 | loop fusion | flops 12058624 | bytes 10502144 | tf_op jit(solution)/shard_map/reduce_sum | solution.py:49
  1062.4 13.0 %psum.47 = f32[2048,1]{0,1:T(1,128)S(1)} all-reduce(f32[2048,1]{0,1:T(1,128)S(1)} %bitcast.50), channel_id=1, replica_groups=mesh['dp'=1,'ffn'=4,'emb'=8] {'emb'}, use_global_device_ids=true, to_apply=%region_16.17 | all-reduce | flops 2048 | bytes 16384 | tf_op jit(solution)/shard_map/psum | solution.py:50
  1075.4 1.4 fusion.21
  (58 shorter events, 6.4 us)
Async XLA Ops:
  6.5 261.0 %copy-start = (bf16[256,64]{0,1:T(8,128)(2,1)S(1)}, bf16[256,64]{0,1:T(8,128)(2,1)}, u32[]{:S(2)}) copy-start(bf16[256,64]{0,1:T(8,128)(2,1)} %param.11) | copy-start | bytes 98308
  6.6 85.4 %copy-start.11 = (bf16[256]{0:T(256)(128)(2,1)S(1)}, bf16[256]{0:T(256)(128)(2,1)}, u32[]{:S(2)}) copy-start(bf16[256]{0:T(256)(128)(2,1)} %param.9) | copy-start | bytes 1540
  6.6 85.4 %copy-start.4 = (bf16[2048,256]{1,0:T(8,128)(2,1)S(1)}, bf16[2048,256]{1,0:T(8,128)(2,1)}, u32[]{:S(2)}) copy-start(bf16[2048,256]{1,0:T(8,128)(2,1)} %param.8) | copy-start | bytes 3145732
  6.6 598.3 %all-reduce.9.cloned.1.call-start = ((), (), s32[]{:S(2)}) async-start(), calls=%async_computation.2 | async-start | bytes 67108864 | tf_op jit(solution)/shard_map/psum | solution.py:43
  30.9 61.0 %copy-start.9 = (s32[16384,1]{0,1:T(1,128)}, s32[16384,1]{0,1:T(1,128)S(1)}, u32[]{:S(2)}) copy-start(s32[16384,1]{0,1:T(1,128)S(1)} %compare_select_fusion) | copy-start | bytes 196612
  235.4 19.2 %copy-start.3 = (bf16[32768,256]{1,0:T(8,128)(2,1)S(1)}, bf16[32768,256]{1,0:T(8,128)(2,1)}, u32[]{:S(2)}) copy-start(bf16[32768,256]{1,0:T(8,128)(2,1)} %gather_fusion) | copy-start | bytes 50331652
  267.5 393.5 %all-reduce.7.cloned.1.call-start = ((), (), s32[]{:S(2)}) async-start(), calls=%async_computation.1 | async-start | bytes 1048576 | tf_op jit(solution)/shard_map/psum | solution.py:37
  268.9 685.9 %all-reduce.5.cloned.1.call-start = ((), (), s32[]{:S(2)}) async-start(), calls=%async_computation | async-start | bytes 33554432 | tf_op jit(solution)/shard_map/psum | solution.py:46
  630.3 0.7 copy-start.12
  630.3 3.1 copy-start.6
  664.4 131.5 %copy-start.7 = (s32[2048,8]{0,1:T(8,128)S(1)}, s32[2048,8]{0,1:T(8,128)}, u32[]{:S(2)}) copy-start(s32[2048,8]{0,1:T(8,128)} %param.15) | copy-start | bytes 196612
  857.5 112.6 %copy-start.2 = (s32[16384]{0:T(1024)S(1)}, s32[16384]{0:T(1024)}, u32[]{:S(2)}) copy-start(s32[16384]{0:T(1024)} %broadcast_clamp_fusion) | copy-start | bytes 196612
  970.1 68.8 %copy-start.8 = (pred[2048,8]{1,0:T(8,128)(4,1)S(1)}, pred[2048,8]{1,0:T(8,128)(4,1)}, u32[]{:S(2)}) copy-start(pred[2048,8]{1,0:T(8,128)(4,1)} %copy.25) | copy-start | bytes 49156
  970.1 106.7 %copy-start.1 = (bf16[256,64]{0,1:T(8,128)(2,1)S(1)}, bf16[256,64]{0,1:T(8,128)(2,1)}, u32[]{:S(2)}) copy-start(bf16[256,64]{0,1:T(8,128)(2,1)} %param.11) | copy-start | bytes 98308
  1038.9 36.5 %copy-start.5 = (bf16[2048,256]{1,0:T(8,128)(2,1)S(1)}, bf16[2048,256]{1,0:T(8,128)(2,1)}, u32[]{:S(2)}) copy-start(bf16[2048,256]{1,0:T(8,128)(2,1)} %param.8) | copy-start | bytes 3145732
  1038.9 36.5 %copy-start.10 = (f32[256]{0:T(256)S(1)}, f32[256]{0:T(256)}, u32[]{:S(2)}) copy-start(f32[256]{0:T(256)} %convert_element_type.62) | copy-start | bytes 3076
Sparse Core Ops, SparseCore 0:
  267.6 337.1 all-reduce.8
  607.2 53.7 all-reduce.6
  663.5 291.1 all-reduce.4
where the time goes:
time: 1080 us
  waiting for transfers between devices  459 us (42%)
  local copies, waits for them, and re-layouts  458 us (42%)
  other arithmetic  68.3 us (6%)
  matrix products  57.5 us (5%)
  blocking collectives  27 us (2%)
  between operations  13.5 us (1%)
    psum x1, waiting for transfers between devices, local_block(): z_gate, z_up = lax.psum((z_gate, z_up), 'emb')  336 us
    gather x5, local copies, waits for them, and re-layouts, route_tokens(): gate_val = jnp.take_along_axis(router_prob, choice, axis=1)  132 us
    gather x1, local copies, waits for them, and re-layouts, local_block(): jnp.take(normed, slot_token, axis=0, mode='fill', fill_value=0)  129 us
    psum x1, waiting for transfers between devices, local_block(): expert_out = lax.psum(part_out, 'ffn')  97.3 us
    gather x1, local copies, waits for them, and re-layouts, local_block(): picked = jnp.take(weighted, position, axis=0, mode='fill', fill_value=0)  68.8 us
    scatter x1, local copies, waits for them, and re-layouts, route_tokens(): jnp.zeros((experts * capacity,), jnp.float32).at[flat_pos]  60.8 us
    scatter x1, local copies, waits for them, and re-layouts, route_tokens(): jnp.full((experts * capacity,), num_tok, jnp.int32).at[flat_pos]  60.4 us
    psum x1, waiting for transfers between devices, local_block(): lax.psum(jnp.dot(normed, w_router, preferred_element_type=jnp.float32), '...  26.1 us
  transfers between devices with their start and end apart: 3, of which 3 were waited for; matrix products, arithmetic and copies ran while one was open for 21% of the time, Pallas kernels for 0%

commit v1 on v0

v1 whole, which is shorter than its diff:
```python
import functools

import jax
import jax.numpy as jnp
from jax import lax
from jax.experimental import pallas as pl
from jax.experimental.pallas import tpu as pltpu
from jax.sharding import PartitionSpec as P

EPS = 1e-5
LANE = 128
F_CHUNKS = 2
ROW_BLOCK = 272
EXPERT_BATCH = 4
VMEM_BYTES = 60 * 1024 * 1024
F32 = jnp.float32
BF16 = jnp.bfloat16


def cost(flops, nbytes):
    return pl.CostEstimate(flops=int(flops), bytes_accessed=int(nbytes), transcendentals=0)


def onehot_pieces(pos_row, rows_hi):
    tokens = pos_row.shape[1]
    hi = jnp.floor(pos_row * (1.0 / LANE))
    lo = pos_row - hi * LANE
    hi_iota = lax.broadcasted_iota(jnp.int32, (rows_hi, tokens), 0).astype(F32)
    lo_iota = lax.broadcasted_iota(jnp.int32, (LANE, tokens), 0).astype(F32)
    return hi == hi_iota, lo == lo_iota


def route_kernel(capacity, experts, choice_ref, tok_ref, seg_ref, pos_ref):
    top_k, tokens = choice_ref.shape
    rows_hi = tok_ref.shape[0]
    rows = rows_hi * LANE
    blk = 256
    e_iota = lax.broadcasted_iota(jnp.int32, (experts, tokens), 0)
    assigned = jnp.zeros((experts, tokens), F32)
    for k in range(top_k):
        assigned += jnp.where(choice_ref[k:k + 1, :] == e_iota, 1.0, 0.0)
    r_i = lax.broadcasted_iota(jnp.int32, (blk, blk), 0)
    c_i = lax.broadcasted_iota(jnp.int32, (blk, blk), 1)
    tri = jnp.where(r_i < c_i, 1.0, 0.0).astype(BF16)
    carry = jnp.zeros((experts, 1), F32)
    before = []
    for b in range(tokens // blk):
        part = assigned[:, b * blk:(b + 1) * blk]
        within = jnp.dot(part.astype(BF16), tri, preferred_element_type=F32)
        before.append(within + carry)
        carry = carry + jnp.sum(part, axis=1, keepdims=True)
    before = jnp.concatenate(before, axis=1)
    kept = jnp.broadcast_to(jnp.minimum(carry, float(capacity)), (experts, LANE))
    kept_hi = jnp.floor(kept * (1.0 / 16.0))
    kept_lo = kept - kept_hi * 16.0
    er = lax.broadcasted_iota(jnp.int32, (experts, experts), 0)
    ec = lax.broadcasted_iota(jnp.int32, (experts, experts), 1)
    low = jnp.where(ec < er, 1.0, 0.0).astype(BF16)
    start = 16.0 * jnp.dot(low, kept_hi.astype(BF16), preferred_element_type=F32)
    start = start + jnp.dot(low, kept_lo.astype(BF16), preferred_element_type=F32)
    end = start + kept
    fill = jnp.zeros((LANE - experts, LANE), F32)
    start_t = jnp.transpose(jnp.concatenate([start, fill], axis=0))
    end_t = jnp.transpose(jnp.concatenate([end, fill], axis=0))
    seg_ref[0:1, :] = start_t[0:1, :].astype(jnp.int32)
    lane = lax.broadcasted_iota(jnp.int32, (1, LANE), 1)
    seg_ref[1:2, :] = jnp.where(lane == experts - 1, rows, end_t[0:1, :].astype(jnp.int32))
    value = jnp.where(before < capacity, before + start[:, 0:1], float(rows))
    t_val = lax.broadcasted_iota(jnp.int32, (1, tokens), 1) + 1
    t_hi = (t_val // 16).astype(F32)
    t_lo = (t_val % 16).astype(F32)
    acc = jnp.zeros((rows_hi, 2 * LANE), F32)
    for k in range(top_k):
        hit = choice_ref[k:k + 1, :] == e_iota
        pos = jnp.sum(jnp.where(hit, value, 0.0), axis=0, keepdims=True)
        pos_ref[k:k + 1, :] = pos
        is_hi, is_lo = onehot_pieces(pos, rows_hi)
        left = jnp.where(is_hi, 1.0, 0.0).astype(BF16)
        right = jnp.concatenate([jnp.where(is_lo, t_hi, 0.0), jnp.where(is_lo, t_lo, 0.0)], axis=0).astype(BF16)
        acc += lax.dot_general(left, right, (((1,), (1,)), ((), ())), preferred_element_type=F32)
    tok_ref[...] = (16.0 * acc[:, :LANE] + acc[:, LANE:]).astype(jnp.int32) - 1


def route(choice, experts, capacity):
    tokens, top_k = choice.shape
    rows_hi = tokens * top_k // LANE
    return pl.pallas_call(
        functools.partial(route_kernel, capacity, experts),
        out_shape=(
            jax.ShapeDtypeStruct((rows_hi, LANE), jnp.int32),
            jax.ShapeDtypeStruct((2, LANE), jnp.int32),
            jax.ShapeDtypeStruct((top_k, tokens), F32),
        ),
        compiler_params=pltpu.CompilerParams(vmem_limit_bytes=VMEM_BYTES),
        cost_estimate=cost(10e9, 1e5),
        name='route',
    )(choice.T)


def norm_kernel(hid_ref, inv_ref, pre_ref, wr_ref, b_ref, logit_ref):
    width = hid_ref.shape[1]
    for i in range(inv_ref.shape[0]):
        col = jnp.concatenate([column_of(inv_ref[i:i + 1, :])] * (width // LANE), axis=1)
        part = slice(i * LANE, (i + 1) * LANE)
        b_ref[part, :] = (hid_ref[part, :].astype(F32) * col * pre_ref[...].astype(F32)).astype(BF16)
    b = b_ref[...]
    logit_ref[...] = lax.dot_general(wr_ref[...], b, (((0,), (1,)), ((), ())), preferred_element_type=F32)


def norm_logits(hidden, inv_pre, norm_pre, w_router):
    tokens, width = hidden.shape
    experts = w_router.shape[1]
    return pl.pallas_call(
        norm_kernel,
        out_shape=(
            jax.ShapeDtypeStruct((tokens, width), BF16),
            jax.ShapeDtypeStruct((experts, tokens), F32),
        ),
        compiler_params=pltpu.CompilerParams(vmem_limit_bytes=VMEM_BYTES),
        cost_estimate=cost(5e9, 3e6),
        name='norm_logits',
    )(hidden, inv_pre.reshape(tokens // LANE, LANE), norm_pre.reshape(1, width), w_router)


def column_of(row):
    return jnp.transpose(jnp.broadcast_to(row, (LANE, LANE)))


def dispatch_kernel(tok_ref, b_ref, x_ref):
    i = pl.program_id(0)
    tokens = b_ref.shape[0]
    rows = x_ref.shape[0]
    lane = lax.broadcasted_iota(jnp.int32, (LANE, LANE), 1)
    strips = []
    for q in range(rows // LANE):
        col = column_of(tok_ref[pl.ds(i * (rows // LANE) + q, 1), :])
        strips.append(jnp.concatenate(
            [jnp.where(col == lane + j * LANE, 1.0, 0.0).astype(BF16) for j in range(tokens // LANE)], axis=1))
    pick = jnp.concatenate(strips, axis=0)
    x_ref[...] = jnp.dot(pick, b_ref[...], preferred_element_type=F32).astype(BF16)


def dispatch(tok, b):
    tokens, width = b.shape
    rows = tok.size
    blk = 512
    return pl.pallas_call(
        dispatch_kernel,
        out_shape=jax.ShapeDtypeStruct((rows, width), BF16),
        grid=(rows // blk,),
        in_specs=[
            pl.BlockSpec(tok.shape, lambda i: (0, 0)),
            pl.BlockSpec((tokens, width), lambda i: (0, 0)),
        ],
        out_specs=pl.BlockSpec((blk, width), lambda i: (i, 0)),
        compiler_params=pltpu.CompilerParams(vmem_limit_bytes=VMEM_BYTES),
        cost_estimate=cost(2 * rows * tokens * width, rows * width * 2),
        name='dispatch',
    )(tok, b)


def grouped(seg_ref, step, in_refs, weights, out_ref):
    total = out_ref.shape[0]
    batch = len(weights)

    def block(e, w, offset):
        s = seg_ref[0, e]
        r0 = pl.multiple_of(jnp.minimum((s // 16) * 16 + offset, total - ROW_BLOCK), 16)
        parts = [r[pl.ds(r0, ROW_BLOCK), :] for r in in_refs]
        src = parts[0] if len(parts) == 1 else jnp.concatenate(parts, axis=1)
        new = jnp.dot(src, w(), preferred_element_type=F32).astype(BF16)
        return s, r0, new

    def put(s, r0, new):
        row = r0 + lax.broadcasted_iota(jnp.int32, new.shape, 0)
        out_ref[pl.ds(r0, ROW_BLOCK), :] = jnp.where(row >= s, new, out_ref[pl.ds(r0, ROW_BLOCK), :])

    long = jnp.bool_(False)
    for q in range(batch):
        e = step * batch + q
        long = jnp.logical_or(long, seg_ref[1, e] - (seg_ref[0, e] // 16) * 16 > ROW_BLOCK)

    @pl.when(jnp.logical_not(long))
    def short_segments():
        for item in [block(step * batch + q, weights[q], 0) for q in range(batch)]:
            put(*item)

    @pl.when(long)
    def long_segments():
        for q in range(batch):
            e = step * batch + q
            count = (seg_ref[1, e] - (seg_ref[0, e] // 16) * 16 + ROW_BLOCK - 1) // ROW_BLOCK

            def body(j, carry):
                put(*block(e, weights[q], j * ROW_BLOCK))
                return carry

            lax.fori_loop(0, count, body, 0)


def up_kernel(seg_ref, x_ref, wg_ref, wu_ref, z_ref):
    pick = lambda q: lambda: jnp.concatenate([wg_ref[q], wu_ref[q]], axis=1)
    grouped(seg_ref, pl.program_id(0), [x_ref], [pick(q) for q in range(wg_ref.shape[0])], z_ref)


def expert_up(seg, x, w_gate, w_up, chunk, chunks):
    rows, width = x.shape
    experts, _, ffn = w_gate.shape
    part = ffn // chunks
    w_spec = pl.BlockSpec((EXPERT_BATCH, width, part), lambda e, seg: (e, 0, chunk))
    return pl.pallas_call(
        up_kernel,
        out_shape=jax.ShapeDtypeStruct((rows, 2 * part), BF16),
        grid_spec=pltpu.PrefetchScalarGridSpec(
            num_scalar_prefetch=1,
            grid=(experts // EXPERT_BATCH,),
            in_specs=[pl.BlockSpec((rows, width), lambda e, seg: (0, 0), pipeline_mode=pl.Buffered(1)), w_spec, w_spec],
            out_specs=pl.BlockSpec((rows, 2 * part), lambda e, seg: (0, 0), pipeline_mode=pl.Buffered(1)),
        ),
        compiler_params=pltpu.CompilerParams(vmem_limit_bytes=VMEM_BYTES),
        cost_estimate=cost(8 * rows * width * part, 4 * rows * width),
        name='expert_up',
    )(seg, x, w_gate, w_up)


def gate_kernel(logit_ref, choice_ref, pos_ref, gate_ref):
    experts, tokens = logit_ref.shape
    top_k = choice_ref.shape[0]
    rows_hi = gate_ref.shape[0]
    logits = logit_ref[...]
    grown = jnp.exp(logits - jnp.max(logits, axis=0, keepdims=True))
    prob = grown / jnp.sum(grown, axis=0, keepdims=True)
    e_iota = lax.broadcasted_iota(jnp.int32, (experts, tokens), 0)
    acc = jnp.zeros((rows_hi, 3 * LANE), F32)
    for k in range(top_k):
        hit = choice_ref[k:k + 1, :] == e_iota
        gate = jnp.sum(jnp.where(hit, prob, 0.0), axis=0, keepdims=True)
        is_hi, is_lo = onehot_pieces(pos_ref[k:k + 1, :], rows_hi)
        left = jnp.where(is_hi, 1.0, 0.0).astype(BF16)
        pieces = []
        rest = gate
        for _ in range(3):
            piece = rest.astype(BF16).astype(F32)
            rest = rest - piece
            pieces.append(jnp.where(is_lo, piece, 0.0).astype(BF16))
        right = jnp.concatenate(pieces, axis=0)
        acc += lax.dot_general(left, right, (((1,), (1,)), ((), ())), preferred_element_type=F32)
    gate_ref[...] = acc[:, :LANE] + acc[:, LANE:2 * LANE] + acc[:, 2 * LANE:]


def gates_of_rows(logits, choice_t, pos):
    top_k, tokens = choice_t.shape
    rows_hi = tokens * top_k // LANE
    return pl.pallas_call(
        gate_kernel,
        out_shape=jax.ShapeDtypeStruct((rows_hi, LANE), F32),
        compiler_params=pltpu.CompilerParams(vmem_limit_bytes=VMEM_BYTES),
        cost_estimate=cost(10e9, 1e5),
        name='gates',
    )(logits, choice_t, pos)


def down_kernel(chunks, seg_ref, tok_ref, gate_ref, *refs):
    g_refs = refs[:chunks]
    w_ref, m_ref, y_ref = refs[chunks:]
    tokens, width = m_ref.shape
    rows = y_ref.shape[0]
    pick = lambda q: lambda: w_ref[q]
    grouped(seg_ref, pl.program_id(0), g_refs, [pick(q) for q in range(w_ref.shape[0])], y_ref)

    @pl.when(pl.program_id(0) == pl.num_programs(0) - 1)
    def combine():
        blk = 512
        t_iota = lax.broadcasted_iota(jnp.int32, (tokens, LANE), 0)
        m_ref[...] = jnp.zeros_like(m_ref)

        def body(i, carry):
            scaled, picks = [], []
            for q in range(blk // LANE):
                hi = i * (blk // LANE) + q
                col = column_of(gate_ref[pl.ds(hi, 1), :])
                col = jnp.concatenate([col] * (width // LANE), axis=1)
                r0 = pl.multiple_of(hi * LANE, LANE)
                scaled.append((y_ref[pl.ds(r0, LANE), :].astype(F32) * col).astype(BF16))
                picks.append(jnp.where(t_iota == tok_ref[pl.ds(hi, 1), :], 1.0, 0.0).astype(BF16))
            u = jnp.concatenate(scaled, axis=0)
            pick = jnp.concatenate(picks, axis=1)
            m_ref[...] += jnp.dot(pick, u, preferred_element_type=F32)
            return carry

        lax.fori_loop(0, rows // blk, body, 0)


def expert_down(seg, tok, gate, acts, w_down, tokens):
    rows, part = acts[0].shape
    experts, ffn, width = w_down.shape
    whole = lambda e, seg: (0, 0)
    one = pl.Buffered(1)
    return pl.pallas_call(
        functools.partial(down_kernel, len(acts)),
        out_shape=jax.ShapeDtypeStruct((tokens, width), F32),
        grid_spec=pltpu.PrefetchScalarGridSpec(
            num_scalar_prefetch=1,
            grid=(experts // EXPERT_BATCH,),
            in_specs=[pl.BlockSpec(tok.shape, whole), pl.BlockSpec(gate.shape, whole)]
            + [pl.BlockSpec((rows, part), whole, pipeline_mode=one) for _ in acts]
            + [pl.BlockSpec((EXPERT_BATCH, ffn, width), lambda e, seg: (e, 0, 0))],
            out_specs=pl.BlockSpec((tokens, width), whole, pipeline_mode=one),
            scratch_shapes=[pltpu.VMEM((rows, width), BF16)],
        ),
        compiler_params=pltpu.CompilerParams(vmem_limit_bytes=VMEM_BYTES),
        cost_estimate=cost(2 * rows * width * (ffn + tokens), 4 * rows * width),
        name='expert_down',
    )(seg, tok, gate, *acts, w_down)


def solution(mesh):
    emb_size = mesh.shape['emb']

    def local_block(hidden, norm_pre, norm_post, w_router, w_gate, w_up, w_down, choice):
        num_tok, local_width = hidden.shape
        model_width = local_width * emb_size
        experts = w_gate.shape[0]
        top_k = choice.shape[1]
        capacity = 2 * num_tok * top_k // experts
        hid_f32 = hidden.astype(F32)
        sq_pre = lax.psum(jnp.sum(hid_f32 * hid_f32, axis=1), 'emb')
        inv_pre = lax.rsqrt(sq_pre / model_width + EPS)
        tok, seg, pos = route(choice, experts, capacity)
        normed, logits = norm_logits(hidden, inv_pre, norm_pre, w_router)
        x = dispatch(tok, normed)
        logits = lax.psum(logits, 'emb')
        x, logits = lax.optimization_barrier((x, logits))
        acts = []
        for c in range(F_CHUNKS):
            z = expert_up(seg, x, w_gate, w_up, c, F_CHUNKS)
            z = lax.psum_scatter(z, 'emb', scatter_dimension=0, tiled=True)
            half = z.shape[1] // 2
            act = (jax.nn.gelu(z[:, :half].astype(F32), approximate=True) * z[:, half:].astype(F32)).astype(BF16)
            acts.append(lax.all_gather(act, 'emb', axis=0, tiled=True))
        gate = gates_of_rows(logits, choice.T, pos)
        mix = expert_down(seg, tok, gate, acts, w_down, num_tok)
        ffn_size = lax.axis_size('ffn')
        mix = lax.psum_scatter(mix, 'ffn', scatter_dimension=0, tiled=True)
        own = num_tok // ffn_size
        hid_own = lax.dynamic_slice_in_dim(hidden, lax.axis_index('ffn') * own, own, 0).astype(F32)
        sq_post = lax.psum(jnp.sum(mix * mix, axis=1), 'emb')[:, None]
        inv_post = lax.rsqrt(sq_post / model_width + EPS)
        out = (hid_own + mix * inv_post * norm_post.astype(F32)).astype(BF16)
        return lax.all_gather(out, 'ffn', axis=0, tiled=True)

    in_specs = (P('dp', 'emb'), P('emb'), P('emb'), P('emb', None), P(None, 'emb', 'ffn'), P(None, 'emb', 'ffn'), P(None, 'ffn', 'emb'), P('dp', None))
    return jax.shard_map(local_block, mesh=mesh, in_specs=in_specs, out_specs=P('dp', 'emb'), check_vma=False)
```

time: 1080 us -> 389 us (0.36)
  local copies, waits for them, and re-layouts: 458 us -> 5 us
  waiting for transfers between devices: 459 us -> 202 us
  Pallas kernels: 0 us -> 127 us
  other arithmetic: 68.3 us -> 10.2 us
  matrix products: 57.5 us -> 0 us
    psum x3 -> x1, waiting for transfers between devices: 459 us -> 23.6 us  [local_block(): logits = lax.psum(logits, 'emb')]
    gather x7 -> x0, local copies, waits for them, and re-layouts: 330 us -> none  [the longest x5 132 us: route_tokens(): gate_val = jnp.take_along_axis(router_prob, choice, axis=1)]
    pallas_call x0 -> x7, Pallas kernels: none -> 127 us  [the longest x1 45.2 us: expert_down(): pl.pallas_call(functools.partial(down_kernel, len(acts)), out_shape=jax.S...]
    scatter x2 -> x0, local copies, waits for them, and re-layouts: 121 us -> none  [the longest x1 60.8 us: route_tokens(): jnp.zeros((experts * capacity,), jnp.float32).at[flat_pos]]
    reduce_scatter x0 -> x3, waiting for transfers between devices: none -> 106 us  [the longest x2 79.8 us: local_block(): z = lax.psum_scatter(z, 'emb', scatter_dimension=0, tiled=True)]
    all_gather x0 -> x3, waiting for transfers between devices: none -> 72 us  [the longest x2 53.6 us: local_block(): acts.append(lax.all_gather(act, 'emb', axis=0, tiled=True))]
    dot_general x4 -> x0, matrix products: 57.5 us -> none  [the longest x1 25.4 us: local_block(): jnp.einsum('ecf,efd->ecd', act_val, w_down, preferred_element_type=jnp.fl...]
    reduce_sum x6 -> x2, other arithmetic: 27.9 us -> 2.76 us  [the longest x1 1.57 us: local_block(): sq_pre = lax.psum(jnp.sum(hid_f32 * hid_f32, axis=1), 'emb')]
  transfers between devices with their start and end apart: 3 -> 7, of which waited for: 3 -> 7; matrix products, arithmetic and copies ran while one was open for 21% -> 1% of each run, Pallas kernels for 0% -> 15%
where the time goes in v1:
time: 389 us; the launch traced here: 385 us
  waiting for transfers between devices  202 us (52%)
  Pallas kernels  127 us (33%)
  blocking collectives  26.8 us (7%)
  between operations  13.6 us (3%)
  other arithmetic  10.2 us (3%)
  local copies, waits for them, and re-layouts  5 us (1%)
    reduce_scatter x2, waiting for transfers between devices, local_block(): z = lax.psum_scatter(z, 'emb', scatter_dimension=0, tiled=True)  79.8 us
    all_gather x2, waiting for transfers between devices, local_block(): acts.append(lax.all_gather(act, 'emb', axis=0, tiled=True))  53.6 us
    pallas_call x1, Pallas kernels, expert_down(): pl.pallas_call(functools.partial(down_kernel, len(acts)), out_shape=jax.S...  45.2 us
    pallas_call x2, Pallas kernels, expert_up(): pl.pallas_call(up_kernel, out_shape=jax.ShapeDtypeStruct((rows, 2 * part)...  40.6 us
    pallas_call x1, Pallas kernels, dispatch(): pl.pallas_call(dispatch_kernel, out_shape=jax.ShapeDtypeStruct((rows, wid...  26.5 us
    reduce_scatter x1, waiting for transfers between devices, local_block(): mix = lax.psum_scatter(mix, 'ffn', scatter_dimension=0, tiled=True)  26.4 us
    psum x1, waiting for transfers between devices, local_block(): logits = lax.psum(logits, 'emb')  23.6 us
    all_gather x1, waiting for transfers between devices, local_block(): return lax.all_gather(out, 'ffn', axis=0, tiled=True)  18.4 us
  transfers between devices with their start and end apart: 7, of which 7 were waited for; matrix products, arithmetic and copies ran while one was open for 1% of the time, Pallas kernels for 15%

profile of v1, /device:TPU:97, one launch (start us, length us, event | category | flops | bytes accessed | tf_op | source)
XLA Modules:
  0.0 385.2 jit_solution(9459510383750299986)
XLA Ops:
  6.6 1.6 multiply_reduce_fusion
  8.1 14.1 %psum.21 = f32[2048]{0:T(1024)S(1)} all-reduce(f32[2048]{0:T(1024)S(1)} %multiply_reduce_fusion), channel_id=1, replica_groups=mesh['dp'=1,'ffn'=4,'emb'=8] {'emb'}, use_global_device_ids=true, to_apply=%region_1.0 | all-reduce | flops 2048 | bytes 16384 | tf_op jit(solution)/shard_map/psum | solution.py:327
  22.2 0.6 rsqrt_bitcast_fusion.inv_ref
  22.8 1.2 reshape.12.pre_ref
  24.0 1.5 copy.9.wr_ref
  25.5 2.8 norm_logits.1
  28.3 0.1 all-reduce.2.cloned.1.call-update
  28.4 0.1 reduce-scatter.4.cloned.1.call-start
  28.5 6.1 %route.1 = (s32[128,128]{1,0:T(8,128)}, s32[2,128]{1,0:T(2,128)}, f32[8,2048]{1,0:T(8,128)}) custom-call(s32[8,2048]{1,0:T(8,128)} %bitcast.3), custom_call_target="tpu_custom_call" | custom-call | flops 10000000000 | bytes 100000 | tf_op jit(solution)/shard_map/route/pallas_call | solution.py:87
  34.6 26.5 %dispatch.1.x_ref = bf16[16384,256]{1,0:T(8,128)(2,1)} custom-call(s32[128,128]{1,0:T(8,128)} %get-tuple-element.13.tok_ref, bf16[2048,256]{1,0:T(8,128)(2,1)} %get-tuple-element.14.b_ref), custom_call_target="tpu_custom_call" | custom-call | flops 17179869184 | bytes 8388608 | tf_op jit(solution)/shard_map/dispatch/pallas_call | solution.py:147
  61.1 23.6 %all-reduce.2.cloned.1.call-done.logit_ref = f32[64,2048]{1,0:T(8,128)} async-done(((f32[64,2048]{1,0:T(8,128)}), f32[64,2048]{1,0:T(8,128)}) %all-reduce.2.cloned.1.call-update) | async-done | bytes 524304 | tf_op jit(solution)/shard_map/psum | solution.py:332
  84.7 20.3 %expert_up.2 = bf16[16384,256]{1,0:T(8,128)(2,1)} custom-call(s32[2,128]{1,0:T(2,128)} %get-tuple-element.12.seg_ref, bf16[16384,256]{1,0:T(8,128)(2,1)} %dispatch.1.x_ref, bf16[64,256,256]{2,1,0:T(8,128)(2,1)} %wg_ref.3, bf16[64,256,256]{2,1,0:T(8,128)(2,1)} %wu_ref.3), custom_call_target="tpu_custom_call" | custom-call | flops 4294967296 | bytes 16777216 | tf_op jit(solution)/shard_map/expert_up/pallas_call | solution.py:211
  105.0 0.1 reduce-scatter.6.cloned.1.call-start
  105.1 20.3 %expert_up.3 = bf16[16384,256]{1,0:T(8,128)(2,1)} custom-call(s32[2,128]{1,0:T(2,128)} %get-tuple-element.12.seg_ref, bf16[16384,256]{1,0:T(8,128)(2,1)} %dispatch.1.x_ref, bf16[64,256,256]{2,1,0:T(8,128)(2,1)} %wg_ref.3, bf16[64,256,256]{2,1,0:T(8,128)(2,1)} %wu_ref.3), custom_call_target="tpu_custom_call" | custom-call | flops 4294967296 | bytes 16777216 | tf_op jit(solution)/shard_map/expert_up/pallas_call | solution.py:211
  125.5 0.1 all-gather.4.cloned.1.call-start
  125.5 30.4 %reduce-scatter.4.cloned.1.call-done = bf16[2048,256]{1,0:T(8,128)(2,1)} async-done(((bf16[16384,256]{1,0:T(8,128)(2,1)}), bf16[2048,256]{1,0:T(8,128)(2,1)}) %reduce-scatter.4.cloned.1.call-update) | async-done | bytes 1048592 | tf_op jit(solution)/shard_map/reduce_scatter | solution.py:337
  155.9 2.4 fusion.6
  158.4 0.1 all-gather.6.cloned.1.call-start
  158.5 49.4 %reduce-scatter.6.cloned.1.call-done = bf16[2048,256]{1,0:T(8,128)(2,1)} async-done(((bf16[16384,256]{1,0:T(8,128)(2,1)}), bf16[2048,256]{1,0:T(8,128)(2,1)}) %reduce-scatter.6.cloned.1.call-update) | async-done | bytes 1048592 | tf_op jit(solution)/shard_map/reduce_scatter | solution.py:337
  207.9 2.4 fusion.13
  210.4 0.2 reduce-scatter.8.cloned.1.call-start
  210.7 5.6 %gates.1.gate_ref = f32[128,128]{1,0:T(8,128)} custom-call(f32[64,2048]{1,0:T(8,128)} %all-reduce.2.cloned.1.call-done.logit_ref, s32[8,2048]{1,0:T(8,128)} %bitcast.4, f32[8,2048]{1,0:T(8,128)} %get-tuple-element.17.pos_ref), custom_call_target="tpu_custom_call" | custom-call | flops 10000000000 | bytes 100000 | tf_op jit(solution)/shard_map/gates/pallas_call | solution.py:254
  216.3 22.9 %all-gather.4.cloned.1.call-done.refs_0_ = bf16[16384,128]{1,0:T(8,128)(2,1)} async-done(((bf16[2048,128]{1,0:T(8,128)(2,1)}), bf16[16384,128]{1,0:T(8,128)(2,1)}) %all-gather.4.cloned.1.call-update) | async-done | bytes 4194320 | tf_op jit(solution)/shard_map/all_gather | solution.py:340
  239.2 30.7 %all-gather.6.cloned.1.call-done.refs_1_ = bf16[16384,128]{1,0:T(8,128)(2,1)} async-done(((bf16[2048,128]{1,0:T(8,128)(2,1)}), bf16[16384,128]{1,0:T(8,128)(2,1)}) %all-gather.6.cloned.1.call-update) | async-done | bytes 4194320 | tf_op jit(solution)/shard_map/all_gather | solution.py:340
  269.9 45.2 %expert_down.1 = f32[2048,256]{1,0:T(8,128)} custom-call(s32[2,128]{1,0:T(2,128)} %get-tuple-element.12.seg_ref, s32[128,128]{1,0:T(8,128)} %get-tuple-element.13.tok_ref, f32[128,128]{1,0:T(8,128)} %gates.1.gate_ref, bf16[16384,128]{1,0:T(8,128)(2,1)} %all-gather.4.cloned.1.call-done.refs_0_, bf16[16384,128]{1,0:T(8,128)(2,1)} %all-gather.6.cloned.1.call-done.refs_1_, ...), custom_call_target="tpu_custom_call" | custom-call | flops 19327352832 | bytes 16777216 | tf_op jit(solution)/shard_map/expert_down/pallas_call | solution.py:299
  315.2 0.1 all-gather.8.cloned.1.call-start
  315.3 26.4 %reduce-scatter.8.cloned.1.call-done = f32[512,256]{1,0:T(8,128)} async-done(((f32[2048,256]{1,0:T(8,128)}), f32[512,256]{1,0:T(8,128)}) %reduce-scatter.8.cloned.1.call-update) | async-done | bytes 524304 | tf_op jit(solution)/shard_map/reduce_scatter | solution.py:344
  341.7 1.2 multiply_reduce_fusion.1
  342.9 12.8 %psum.23 = f32[512]{0:T(512)S(1)} all-reduce(f32[512]{0:T(512)S(1)} %multiply_reduce_fusion.1), channel_id=1, replica_groups=mesh['dp'=1,'ffn'=4,'emb'=8] {'emb'}, use_global_device_ids=true, to_apply=%region_7.0 | all-reduce | flops 512 | bytes 4096 | tf_op jit(solution)/shard_map/psum | solution.py:347
  355.7 2.0 add_convert_fusion
  357.7 18.4 %all-gather.8.cloned.1.call-done = bf16[2048,256]{1,0:T(8,128)(2,1)} async-done(((bf16[512,256]{1,0:T(8,128)(2,1)}), bf16[2048,256]{1,0:T(8,128)(2,1)}) %all-gather.8.cloned.1.call-update) | async-done | bytes 1048592 | tf_op jit(solution)/shard_map/all_gather | solution.py:350
  376.1 2.3 copy.12
  (11 shorter events, 0.3 us)
Async XLA Ops:
  6.5 78.1 %all-reduce.2.cloned.1.call-start = ((), (), s32[]{:S(2)}) async-start(), calls=%async_computation.3 | async-start | bytes 1048576 | tf_op jit(solution)/shard_map/psum | solution.py:332
  28.4 127.6 %reduce-scatter.4.cloned.1.call-start = ((), (), s32[]{:S(2)}) async-start(), calls=%async_computation.4 | async-start | bytes 9437184 | tf_op jit(solution)/shard_map/reduce_scatter | solution.py:337
  105.0 102.9 %reduce-scatter.6.cloned.1.call-start = ((), (), s32[]{:S(2)}) async-start(), calls=%async_computation.6 | async-start | bytes 9437184 | tf_op jit(solution)/shard_map/reduce_scatter | solution.py:337
  125.5 113.8 %all-gather.4.cloned.1.call-start = ((), (), s32[]{:S(2)}) async-start(), calls=%async_computation.5 | async-start | bytes 4718592 | tf_op jit(solution)/shard_map/all_gather | solution.py:340
  158.4 111.5 %all-gather.6.cloned.1.call-start = ((), (), s32[]{:S(2)}) async-start(), calls=%async_computation.7 | async-start | bytes 4718592 | tf_op jit(solution)/shard_map/all_gather | solution.py:340
  210.4 131.3 %reduce-scatter.8.cloned.1.call-start = ((), (), s32[]{:S(2)}) async-start(), calls=%async_computation.8 | async-start | bytes 2621440 | tf_op jit(solution)/shard_map/reduce_scatter | solution.py:344
  216.3 98.9 %copy-start = (bf16[256]{0:T(256)(128)(2,1)S(1)}, bf16[256]{0:T(256)(128)(2,1)}, u32[]{:S(2)}) copy-start(bf16[256]{0:T(256)(128)(2,1)} %param.10) | copy-start | bytes 1540
  315.2 61.0 %all-gather.8.cloned.1.call-start = ((), (), s32[]{:S(2)}) async-start(), calls=%async_computation.9 | async-start | bytes 1310720 | tf_op jit(solution)/shard_map/all_gather | solution.py:350
Sparse Core Ops, SparseCore 0:
  28.5 56.1 all-reduce.1
  105.2 50.7 reduce-scatter.3
  158.3 49.6 reduce-scatter.5
  209.4 29.7 all-gather.3
  240.7 29.1 all-gather.5
  315.3 26.3 reduce-scatter.7
  357.8 18.2 all-gather.7

commit v2 on v1

--- a/solution.py
+++ b/solution.py
@@ -9,16 +9,25 @@
 
 EPS = 1e-5
 LANE = 128
-F_CHUNKS = 2
 ROW_BLOCK = 272
 EXPERT_BATCH = 4
 VMEM_BYTES = 60 * 1024 * 1024
 F32 = jnp.float32
 BF16 = jnp.bfloat16
+MESH = pl.DeviceIdType.MESH
 
 
 def cost(flops, nbytes):
     return pl.CostEstimate(flops=int(flops), bytes_accessed=int(nbytes), transcendentals=0)
+
+
+def greet(peers):
+    barrier = pltpu.get_barrier_semaphore()
+    count = 0
+    for peer in peers:
+        pl.semaphore_signal(barrier, inc=1, device_id=peer, device_id_type=MESH)
+        count += 1
+    pl.semaphore_wait(barrier, count)
 
 
 def onehot_pieces(pos_row, rows_hi):
@@ -223,22 +232,199 @@
     )(seg, x, w_gate, w_up)
 
 
-def gate_kernel(logit_ref, choice_ref, pos_ref, gate_ref):
+def exchange_kernel(emb_size, subs, z_ref, g_ref, mine, theirs, ring, load, send_p, recv_p, send_r, recv_r,
+                    send_a, recv_a, send_d, recv_d):
+    chips = emb_size // 2
+    last = chips - 1
+    me = lax.axis_index('emb')
+    chip, core = me // 2, lax.rem(me, 2)
+    partner = {'emb': chip * 2 + 1 - core}
+    ways = [{'emb': lax.rem(me + 2, emb_size)}, {'emb': lax.rem(me + emb_size - 2, emb_size)}]
+    own = z_ref.shape[0] // emb_size
+    half = own // 2
+    sub = half // subs
+    ffn = g_ref.shape[1]
+    greet([partner] + ways)
+
+    def around(c):
+        return lax.rem(c + 2 * chips, chips)
+
+    def target(d, step):
+        return around(chip - 1 - step if d == 0 else chip + 1 + step)
+
+    def rows(c, parity, d, u, size):
+        return pl.ds(pl.multiple_of((c * 2 + parity) * own + d * half + u * sub, sub), size)
+
+    order = [(step, u, d) for step in range(chips) for u in range(subs) for d in range(2)]
+    loads, passed, sums = {}, {}, {}
+    for step, u, d in order:
+        c = target(d, step)
+        copy = pltpu.make_async_remote_copy(
+            src_ref=z_ref.at[rows(c, 1 - core, d, u, sub), :], dst_ref=theirs.at[step, d, u],
+            send_sem=send_p.at[step, d, u], recv_sem=recv_p.at[step, d, u],
+            device_id=partner, device_id_type=MESH)
+        copy.start()
+        passed[step, d, u] = copy
+        copy = pltpu.make_async_copy(z_ref.at[rows(c, core, d, u, sub), :], mine.at[step, d, u], load.at[step, d, u])
+        copy.start()
+        loads[step, d, u] = copy
+
+    spread = {}
+
+    def scatter(d, way, step, c, u):
+        at = rows(c, core, d, u, sub)
+        copy = pltpu.make_async_remote_copy(
+            src_ref=g_ref.at[at, :], dst_ref=g_ref.at[at, :],
+            send_sem=send_a.at[way, step, d, u], recv_sem=recv_a.at[way, step, d, u],
+            device_id=ways[way], device_id_type=MESH)
+        copy.start()
+        spread[way, step, d, u] = copy
+
+    across = {}
+
+    def share(d, slot, c, u):
+        at = rows(c, core, d, u, sub)
+        copy = pltpu.make_async_remote_copy(
+            src_ref=g_ref.at[at, :], dst_ref=g_ref.at[at, :],
+            send_sem=send_d.at[slot, d, u], recv_sem=recv_d.at[slot, d, u],
+            device_id=partner, device_id_type=MESH)
+        copy.start()
+        across[slot, d, u] = copy
+
+    def sends(way, step, d):
+        if step < (chips - 1) // 2:
+            return True
+        return step == (chips - 1) // 2 and chips % 2 == 0 and way == d
+
+    piece = 32
+    for step, u, d in order:
+        loads[step, d, u].wait()
+        passed[step, d, u].wait_recv()
+        if step >= 1:
+            sums[step - 1, d, u].wait_recv()
+        if step < last:
+            def add(i, carry):
+                at = pl.ds(pl.multiple_of(i * piece, piece), piece)
+                v = mine[step, d, u, at, :].astype(F32) + theirs[step, d, u, at, :].astype(F32)
+                if step >= 1:
+                    v = v + ring[step - 1, d, u, at, :].astype(F32)
+                mine[step, d, u, at, :] = v.astype(BF16)
+                return carry
+
+            lax.fori_loop(0, sub // piece, add, 0)
+            copy = pltpu.make_async_remote_copy(
+                src_ref=mine.at[step, d, u], dst_ref=ring.at[step, d, u],
+                send_sem=send_r.at[step, d, u], recv_sem=recv_r.at[step, d, u],
+                device_id=ways[d], device_id_type=MESH)
+            copy.start()
+            sums[step, d, u] = copy
+        else:
+            def act(i, carry):
+                at = pl.ds(pl.multiple_of(i * piece, piece), piece)
+                v = mine[step, d, u, at, :].astype(F32) + theirs[step, d, u, at, :].astype(F32)
+                v = (v + ring[step - 1, d, u, at, :].astype(F32)).astype(BF16).astype(F32)
+                v = jax.nn.gelu(v[:, :ffn], approximate=True) * v[:, ffn:]
+                out = pl.ds(pl.multiple_of((chip * 2 + core) * own + d * half + u * sub + i * piece, piece), piece)
+                g_ref[out, :] = v.astype(BF16)
+                return carry
+
+            lax.fori_loop(0, sub // piece, act, 0)
+            for way in range(2):
+                if sends(way, 0, d):
+                    scatter(d, way, 0, chip, u)
+            share(d, 0, chip, u)
+    slot = 0
+    for step in range(chips // 2):
+        for u in range(subs):
+            for way in range(2):
+                for d in range(2):
+                    if sends(way, step, d):
+                        spread[way, step, d, u].wait_recv()
+                        c = around(chip - 1 - step if way == 0 else chip + 1 + step)
+                        if sends(way, step + 1, d):
+                            scatter(d, way, step + 1, c, u)
+                        full = sends(0, step, d) and sends(1, step, d)
+                        share(d, 1 + 2 * step + (way if full else 0), c, u)
+    for copy in across.values():
+        copy.wait_recv()
+    for group in (passed, sums, spread, across):
+        for copy in group.values():
+            copy.wait_send()
+
+
+def exchange(z, emb_size):
+    rows, both = z.shape
+    chips = emb_size // 2
+    own = rows // emb_size
+    subs = 4
+    sub = own // (2 * subs)
+    dma = pltpu.SemaphoreType.DMA
+    part = (chips, 2, subs)
+    hop = (chips - 1, 2, subs)
+    fan = (2, max(chips // 2, 1), 2, subs)
+    return pl.pallas_call(
+        functools.partial(exchange_kernel, emb_size, subs),
+        out_shape=jax.ShapeDtypeStruct((rows, both // 2), BF16),
+        in_specs=[pl.BlockSpec(memory_space=pl.ANY)],
+        out_specs=pl.BlockSpec(memory_space=pltpu.VMEM),
+        scratch_shapes=[
+            pltpu.VMEM(part + (sub, both), BF16),
+            pltpu.VMEM(part + (sub, both), BF16),
+            pltpu.VMEM(hop + (sub, both), BF16),
+            dma(part), dma(part), dma(part), dma(hop), dma(hop), dma(fan), dma(fan), dma(part), dma(part),
+        ],
+        compiler_params=pltpu.CompilerParams(collective_id=2, has_side_effects=True, vmem_limit_bytes=VMEM_BYTES),
+        cost_estimate=cost(100e9, 4 * rows * both),
+        name='exchange',
+    )(z)
+
+
+def gate_kernel(emb_size, logit_ref, choice_ref, pos_ref, gate_ref, got, gates, send_a, recv_a, send_b, recv_b):
     experts, tokens = logit_ref.shape
     top_k = choice_ref.shape[0]
     rows_hi = gate_ref.shape[0]
-    logits = logit_ref[...]
+    own = tokens // emb_size
+    me = lax.axis_index('emb')
+    greet({'emb': lax.rem(me + j, emb_size)} for j in range(1, emb_size))
+
+    def columns(who):
+        return pl.ds(pl.multiple_of(who * own, own), own)
+
+    parts = []
+    for j in range(1, emb_size):
+        peer = lax.rem(me + j, emb_size)
+        parts.append(pltpu.make_async_remote_copy(
+            src_ref=logit_ref.at[:, columns(peer)], dst_ref=got.at[j - 1],
+            send_sem=send_a.at[j - 1], recv_sem=recv_a.at[j - 1],
+            device_id={'emb': peer}, device_id_type=MESH))
+        parts[-1].start()
+    logits = logit_ref[:, columns(me)]
+    for j in range(1, emb_size):
+        parts[j - 1].wait_recv()
+        logits = logits + got[j - 1]
     grown = jnp.exp(logits - jnp.max(logits, axis=0, keepdims=True))
     prob = grown / jnp.sum(grown, axis=0, keepdims=True)
-    e_iota = lax.broadcasted_iota(jnp.int32, (experts, tokens), 0)
+    e_iota = lax.broadcasted_iota(jnp.int32, (experts, own), 0)
+    mine = choice_ref[:, columns(me)]
+    for k in range(top_k):
+        gates[k:k + 1, columns(me)] = jnp.sum(jnp.where(mine[k:k + 1, :] == e_iota, prob, 0.0), axis=0, keepdims=True)
+    picked = []
+    for j in range(1, emb_size):
+        picked.append(pltpu.make_async_remote_copy(
+            src_ref=gates.at[:, columns(me)], dst_ref=gates.at[:, columns(me)],
+            send_sem=send_b.at[j - 1], recv_sem=recv_b.at[j - 1],
+            device_id={'emb': lax.rem(me + j, emb_size)}, device_id_type=MESH))
+        picked[-1].start()
+    for copy in parts:
+        copy.wait_send()
+    for copy in picked:
+        copy.wait()
     acc = jnp.zeros((rows_hi, 3 * LANE), F32)
     for k in range(top_k):
-        hit = choice_ref[k:k + 1, :] == e_iota
-        gate = jnp.sum(jnp.where(hit, prob, 0.0), axis=0, keepdims=True)
         is_hi, is_lo = onehot_pieces(pos_ref[k:k + 1, :], rows_hi)
         left = jnp.where(is_hi, 1.0, 0.0).astype(BF16)
         pieces = []
-        rest = gate
+        rest = gates[k:k + 1, :]
         for _ in range(3):
             piece = rest.astype(BF16).astype(F32)
             rest = rest - piece
@@ -248,16 +434,143 @@
     gate_ref[...] = acc[:, :LANE] + acc[:, LANE:2 * LANE] + acc[:, 2 * LANE:]
 
 
-def gates_of_rows(logits, choice_t, pos):
+def gates_of_rows(logits, choice_t, pos, emb_size):
     top_k, tokens = choice_t.shape
+    experts = logits.shape[0]
     rows_hi = tokens * top_k // LANE
-    return pl.pallas_call(
-        gate_kernel,
+    others = emb_size - 1
+    dma = pltpu.SemaphoreType.DMA((others,))
+    vmem = pl.BlockSpec(memory_space=pltpu.VMEM)
+    return pl.pallas_call(
+        functools.partial(gate_kernel, emb_size),
         out_shape=jax.ShapeDtypeStruct((rows_hi, LANE), F32),
-        compiler_params=pltpu.CompilerParams(vmem_limit_bytes=VMEM_BYTES),
-        cost_estimate=cost(10e9, 1e5),
+        in_specs=[vmem, vmem, vmem],
+        out_specs=vmem,
+        scratch_shapes=[
+            pltpu.VMEM((others, experts, tokens // emb_size), F32),
+            pltpu.VMEM((top_k, tokens), F32),
+            dma, dma, dma, dma,
+        ],
+        compiler_params=pltpu.CompilerParams(collective_id=0, has_side_effects=True),
+        cost_estimate=cost(15e9, 1e6),
         name='gates',
     )(logits, choice_t, pos)
+
+
+def finish_kernel(ffn_size, emb_size, model_width, mix_ref, hid_ref, post_ref, out_ref, got, total, squares,
+                  send_a, recv_a, send_b, recv_b, send_c, recv_c):
+    tokens, width = mix_ref.shape
+    own = tokens // ffn_size
+    half = width // 2
+    subs = got.shape[2]
+    sub = own // subs
+    me = lax.axis_index('ffn')
+    emb = lax.axis_index('emb')
+    right, left = lax.rem(me + 1, ffn_size), lax.rem(me + ffn_size - 1, ffn_size)
+    peers = [{'ffn': right}, {'ffn': left}]
+    greet(peers + [{'emb': lax.rem(emb + j, emb_size)} for j in range(1, emb_size)])
+
+    def mix_part(d, step, u):
+        chunk = me - 1 - step if d == 0 else me + 1 + step
+        chunk = lax.rem(chunk + ffn_size * 2, ffn_size)
+        row = pl.multiple_of(chunk * own + u * sub, sub)
+        return mix_ref.at[pl.ds(row, sub), d * half:(d + 1) * half]
+
+    sums = {}
+
+    def send(d, step, u):
+        copy = pltpu.make_async_remote_copy(
+            src_ref=mix_part(d, 0, u) if step == 0 else got.at[d, step - 1, u], dst_ref=got.at[d, step, u],
+            send_sem=send_a.at[d, step, u], recv_sem=recv_a.at[d, step, u],
+            device_id=peers[d], device_id_type=MESH)
+        copy.start()
+        sums[d, step, u] = copy
+
+    for u in range(subs):
+        for d in range(2):
+            send(d, 0, u)
+    for step in range(1, ffn_size):
+        for u in range(subs):
+            for d in range(2):
+                sums[d, step - 1, u].wait_recv()
+                if step < ffn_size - 1:
+                    got[d, step - 1, u] = got[d, step - 1, u] + mix_part(d, step, u)[...]
+                    send(d, step, u)
+                else:
+                    total[u * sub:(u + 1) * sub, d * half:(d + 1) * half] = got[d, step - 1, u] + mix_part(d, step, u)[...]
+    for i in range(own // LANE):
+        part = total[i * LANE:(i + 1) * LANE, :]
+        part = part * part
+        lanes = part[:, :LANE]
+        for j in range(1, width // LANE):
+            lanes = lanes + part[:, j * LANE:(j + 1) * LANE]
+        squares[emb_size - 1, i:i + 1, :] = jnp.sum(jnp.transpose(lanes), axis=0, keepdims=True)
+    shares = []
+    for j in range(1, emb_size):
+        shares.append(pltpu.make_async_remote_copy(
+            src_ref=squares.at[emb_size - 1], dst_ref=squares.at[j - 1],
+            send_sem=send_b.at[j - 1], recv_sem=recv_b.at[j - 1],
+            device_id={'emb': lax.rem(emb + j, emb_size)}, device_id_type=MESH))
+        shares[-1].start()
+    for copy in shares:
+        copy.wait_recv()
+    whole = squares[emb_size - 1]
+    for j in range(emb_size - 1):
+        whole = whole + squares[j]
+    inv = lax.rsqrt(whole / model_width + EPS)
+    post = post_ref[...].astype(F32)
+
+    def rows(chunk, start, size):
+        chunk = lax.rem(chunk + ffn_size * 2, ffn_size)
+        return pl.ds(pl.multiple_of(chunk * own + start, size), size)
+
+    for i in range(own // LANE):
+        col = jnp.concatenate([column_of(inv[i:i + 1, :])] * (width // LANE), axis=1)
+        at = rows(me, i * LANE, LANE)
+        out_ref[at, :] = (hid_ref[at, :].astype(F32) + total[i * LANE:(i + 1) * LANE, :] * col * post).astype(BF16)
+    spread = []
+    for step in range(ffn_size // 2):
+        if step >= 1:
+            for copy in spread[-2:]:
+                copy.wait_recv()
+        last = step == (ffn_size - 1) // 2
+        for d in range(2):
+            chunk = me - step if d == 0 else me + step
+            at = rows(chunk, d * own // 2, own // 2) if last else rows(chunk, 0, own)
+            spread.append(pltpu.make_async_remote_copy(
+                src_ref=out_ref.at[at, :], dst_ref=out_ref.at[at, :],
+                send_sem=send_c.at[d, step], recv_sem=recv_c.at[d, step],
+                device_id=peers[d], device_id_type=MESH))
+            spread[-1].start()
+    for copy in spread[-2:]:
+        copy.wait_recv()
+    for copy in list(sums.values()) + shares + spread:
+        copy.wait_send()
+
+
+def finish(mix, hidden, norm_post, ffn_size, emb_size):
+    tokens, width = mix.shape
+    own = tokens // ffn_size
+    subs = 2 if own % 256 == 0 else 1
+    vmem = pl.BlockSpec(memory_space=pltpu.VMEM)
+    dma = pltpu.SemaphoreType.DMA
+    return pl.pallas_call(
+        functools.partial(finish_kernel, ffn_size, emb_size, width * emb_size),
+        out_shape=jax.ShapeDtypeStruct((tokens, width), BF16),
+        in_specs=[vmem, vmem, vmem],
+        out_specs=vmem,
+        scratch_shapes=[
+            pltpu.VMEM((2, ffn_size - 1, subs, own // subs, width // 2), F32),
+            pltpu.VMEM((own, width), F32),
+            pltpu.VMEM((emb_size, own // LANE, LANE), F32),
+            dma((2, ffn_size - 1, subs)), dma((2, ffn_size - 1, subs)),
+            dma((emb_size - 1,)), dma((emb_size - 1,)),
+            dma((2, ffn_size // 2)), dma((2, ffn_size // 2)),
+        ],
+        compiler_params=pltpu.CompilerParams(collective_id=1, has_side_effects=True),
+        cost_estimate=cost(30e9, 8e6),
+        name='finish',
+    )(mix, hidden, norm_post.reshape(1, width))
 
 
 def down_kernel(chunks, seg_ref, tok_ref, gate_ref, *refs):
@@ -316,6 +629,7 @@
 
 def solution(mesh):
     emb_size = mesh.shape['emb']
+    ffn_size = mesh.shape['ffn']
 
     def local_block(hidden, norm_pre, norm_post, w_router, w_gate, w_up, w_down, choice):
         num_tok, local_width = hidden.shape
@@ -329,25 +643,11 @@
         tok, seg, pos = route(choice, experts, capacity)
         normed, logits = norm_logits(hidden, inv_pre, norm_pre, w_router)
         x = dispatch(tok, normed)
-        logits = lax.psum(logits, 'emb')
-        x, logits = lax.optimization_barrier((x, logits))
-        acts = []
-        for c in range(F_CHUNKS):
-            z = expert_up(seg, x, w_gate, w_up, c, F_CHUNKS)
-            z = lax.psum_scatter(z, 'emb', scatter_dimension=0, tiled=True)
-            half = z.shape[1] // 2
-            act = (jax.nn.gelu(z[:, :half].astype(F32), approximate=True) * z[:, half:].astype(F32)).astype(BF16)
-            acts.append(lax.all_gather(act, 'emb', axis=0, tiled=True))
-        gate = gates_of_rows(logits, choice.T, pos)
-        mix = expert_down(seg, tok, gate, acts, w_down, num_tok)
-        ffn_size = lax.axis_size('ffn')
-        mix = lax.psum_scatter(mix, 'ffn', scatter_dimension=0, tiled=True)
-        own = num_tok // ffn_size
-        hid_own = lax.dynamic_slice_in_dim(hidden, lax.axis_index('ffn') * own, own, 0).astype(F32)
-        sq_post = lax.psum(jnp.sum(mix * mix, axis=1), 'emb')[:, None]
-        inv_post = lax.rsqrt(sq_post / model_width + EPS)
-        out = (hid_own + mix * inv_post * norm_post.astype(F32)).astype(BF16)
-        return lax.all_gather(out, 'ffn', axis=0, tiled=True)
+        z = expert_up(seg, x, w_gate, w_up, 0, 1)
+        act = exchange(z, emb_size)
+        gate = gates_of_rows(logits, choice.T, pos, emb_size)
+        mix = expert_down(seg, tok, gate, [act], w_down, num_tok)
+        return finish(mix, hidden, norm_post, ffn_size, emb_size)
 
     in_specs = (P('dp', 'emb'), P('emb'), P('emb'), P('emb', None), P(None, 'emb', 'ffn'), P(None, 'emb', 'ffn'), P(None, 'ffn', 'emb'), P('dp', None))
     return jax.shard_map(local_block, mesh=mesh, in_specs=in_specs, out_specs=P('dp', 'emb'), check_vma=False)

time: 389 us -> 306 us (0.79)
  waiting for transfers between devices: 202 us -> 0 us
  Pallas kernels: 127 us -> 285 us
  between operations: 13.6 us -> 0.06 us
  blocking collectives: 26.8 us -> 14.1 us
  other arithmetic: 10.2 us -> 0.95 us
    pallas_call x1 -> x3, Pallas kernels: 5.64 us -> 178 us  [the longest x1 114 us: exchange(): pl.pallas_call(functools.partial(exchange_kernel, emb_size, subs), out_sh...]
    reduce_scatter x3 -> x0, waiting for transfers between devices: 106 us -> none  [the longest x2 79.8 us: local_block(): z = lax.psum_scatter(z, 'emb', scatter_dimension=0, tiled=True)]
    all_gather x3 -> x0, waiting for transfers between devices: 72 us -> none  [the longest x2 53.6 us: local_block(): acts.append(lax.all_gather(act, 'emb', axis=0, tiled=True))]
    psum x1 -> x0, waiting for transfers between devices: 23.6 us -> none  [local_block(): logits = lax.psum(logits, 'emb')]
    pallas_call x2 -> x1, Pallas kernels: 40.6 us -> 25.9 us  [expert_up(): pl.pallas_call(up_kernel, out_shape=jax.ShapeDtypeStruct((rows, 2 * part)...]
    psum x1 -> x0, blocking collectives: 12.8 us -> none  [local_block(): sq_post = lax.psum(jnp.sum(mix * mix, axis=1), 'emb')[:, None]]
    convert_element_type x4 -> x0, other arithmetic: 6.84 us -> none  [the longest x2 4.87 us: local_block(): (jax.nn.gelu(z[:, :half].astype(F32), approximate=True) * z[:, half:].ast...]
  transfers between devices with their start and end apart: 7 -> 0, of which waited for: 7 -> 0; matrix products, arithmetic and copies ran while one was open for 1% -> 0% of each run, Pallas kernels for 15% -> 0%
where the time goes in v2:
time: 306 us; the launch traced here: 304 us
  Pallas kernels  285 us (93%)
  blocking collectives  14.1 us (5%)
  local copies, waits for them, and re-layouts  4.16 us (1%)
    pallas_call x1, Pallas kernels, exchange(): pl.pallas_call(functools.partial(exchange_kernel, emb_size, subs), out_sh...  114 us
    pallas_call x1, Pallas kernels, expert_down(): pl.pallas_call(functools.partial(down_kernel, len(acts)), out_shape=jax.S...  45.6 us
    pallas_call x1, Pallas kernels, finish(): pl.pallas_call(functools.partial(finish_kernel, ffn_size, emb_size, width...  43 us
    pallas_call x1, Pallas kernels, dispatch(): pl.pallas_call(dispatch_kernel, out_shape=jax.ShapeDtypeStruct((rows, wid...  26.7 us
    pallas_call x1, Pallas kernels, expert_up(): pl.pallas_call(up_kernel, out_shape=jax.ShapeDtypeStruct((rows, 2 * part)...  25.9 us
    pallas_call x1, Pallas kernels, gates_of_rows(): pl.pallas_call(functools.partial(gate_kernel, emb_size), out_shape=jax.Sh...  20.8 us
    psum x1, blocking collectives, local_block(): sq_pre = lax.psum(jnp.sum(hid_f32 * hid_f32, axis=1), 'emb')  14.1 us
    pallas_call x1, Pallas kernels, route(): pl.pallas_call(functools.partial(route_kernel, capacity, experts), out_sh...  6.23 us

profile of v2, /device:TPU:97, one launch (start us, length us, event | category | flops | bytes accessed | tf_op | source)
XLA Modules:
  0.0 304.4 jit_solution(14367910865990462950)
XLA Ops:
  0.0 0.0 copy-start
  0.0 0.0 copy-start.2
  0.0 0.0 copy-start.1
  0.0 6.2 %route.1 = (s32[128,128]{1,0:T(8,128)}, s32[2,128]{1,0:T(2,128)}, f32[8,2048]{1,0:T(8,128)}) custom-call(s32[8,2048]{1,0:T(8,128)} %bitcast.3), custom_call_target="tpu_custom_call" | custom-call | flops 10000000000 | bytes 100000 | tf_op jit(solution)/shard_map/route/pallas_call | solution.py:96
  6.2 0.0 copy-done
  6.2 0.3 multiply_reduce_fusion
  6.6 14.1 %psum.7 = f32[2048]{0:T(1024)S(1)} all-reduce(f32[2048]{0:T(1024)S(1)} %multiply_reduce_fusion), channel_id=1, replica_groups=mesh['dp'=1,'ffn'=4,'emb'=8] {'emb'}, use_global_device_ids=true, to_apply=%region_1.0 | all-reduce | flops 2048 | bytes 16384 | tf_op jit(solution)/shard_map/psum | solution.py:641
  20.7 0.6 rsqrt_bitcast_fusion.inv_ref
  21.3 0.0 copy-done.2
  21.3 0.6 reshape.10.pre_ref
  21.9 0.0 copy-done.1
  21.9 0.7 copy.9.wr_ref
  22.6 2.8 norm_logits.1
  25.4 20.8 %gates.1.gate_ref = f32[128,128]{1,0:T(8,128)} custom-call(f32[64,2048]{1,0:T(8,128)} %get-tuple-element.12.logit_ref, s32[8,2048]{1,0:T(8,128)} %bitcast.4, f32[8,2048]{1,0:T(8,128)} %get-tuple-element.13.pos_ref), custom_call_target="tpu_custom_call" | custom-call | flops 15000000512 | bytes 1000000 | tf_op jit(solution)/shard_map/gates/pallas_call | solution.py:444
  46.2 26.7 %dispatch.1.x_ref = bf16[16384,256]{1,0:T(8,128)(2,1)} custom-call(s32[128,128]{1,0:T(8,128)} %get-tuple-element.11.tok_ref, bf16[2048,256]{1,0:T(8,128)(2,1)} %get-tuple-element.14.b_ref), custom_call_target="tpu_custom_call" | custom-call | flops 17179869184 | bytes 8388608 | tf_op jit(solution)/shard_map/dispatch/pallas_call | solution.py:156
  72.9 25.9 %expert_up.1.z_ref = bf16[16384,512]{1,0:T(8,128)(2,1)} custom-call(s32[2,128]{1,0:T(2,128)} %get-tuple-element.10.seg_ref, bf16[16384,256]{1,0:T(8,128)(2,1)} %dispatch.1.x_ref, bf16[64,256,256]{2,1,0:T(8,128)(2,1)} %wg_ref.1, bf16[64,256,256]{2,1,0:T(8,128)(2,1)} %wu_ref.1), custom_call_target="tpu_custom_call" | custom-call | flops 8589934592 | bytes 16777216 | tf_op jit(solution)/shard_map/expert_up/pallas_call | solution.py:220
  98.8 114.1 %exchange.1.refs_0_ = bf16[16384,256]{1,0:T(8,128)(2,1)} custom-call(bf16[16384,512]{1,0:T(8,128)(2,1)} %expert_up.1.z_ref), custom_call_target="tpu_custom_call" | custom-call | flops 99999997952 | bytes 33554432 | tf_op jit(solution)/shard_map/exchange/pallas_call | solution.py:365
  212.9 0.0 copy-start.3
  213.0 45.6 %expert_down.1.mix_ref = f32[2048,256]{1,0:T(8,128)} custom-call(s32[2,128]{1,0:T(2,128)} %get-tuple-element.10.seg_ref, s32[128,128]{1,0:T(8,128)} %get-tuple-element.11.tok_ref, f32[128,128]{1,0:T(8,128)} %gates.1.gate_ref, bf16[16384,256]{1,0:T(8,128)(2,1)} %exchange.1.refs_0_, bf16[64,256,256]{2,1,0:T(8,128)(2,1)} %refs_1_.1), custom_call_target="tpu_custom_call" | custom-call | flops 19327352832 | bytes 16777216 | tf_op jit(solution)/shard_map/expert_down/pallas_call | solution.py:612
  258.6 0.0 copy-done.3
  258.6 0.6 reshape.11.post_ref
  259.2 43.0 %finish.1 = bf16[2048,256]{1,0:T(8,128)(2,1)} custom-call(f32[2048,256]{1,0:T(8,128)} %expert_down.1.mix_ref, bf16[2048,256]{1,0:T(8,128)(2,1)} %hid_ref.3, bf16[1,256]{1,0:T(2,128)(2,1)} %reshape.11.post_ref), custom_call_target="tpu_custom_call" | custom-call | flops 30000001024 | bytes 8000000 | tf_op jit(solution)/shard_map/finish/pallas_call | solution.py:557
  302.1 2.3 copy.11
Async XLA Ops:
  0.0 6.2 %copy-start = (bf16[2048,256]{1,0:T(8,128)(2,1)S(1)}, bf16[2048,256]{1,0:T(8,128)(2,1)}, u32[]{:S(2)}) copy-start(bf16[2048,256]{1,0:T(8,128)(2,1)} %hid_ref.3) | copy-start | bytes 3145732
  0.0 21.3 %copy-start.2 = (bf16[256]{0:T(256)(128)(2,1)S(1)}, bf16[256]{0:T(256)(128)(2,1)}, u32[]{:S(2)}) copy-start(bf16[256]{0:T(256)(128)(2,1)} %param.9) | copy-start | bytes 1540
  0.0 21.9 %copy-start.1 = (bf16[256,64]{0,1:T(8,128)(2,1)S(1)}, bf16[256,64]{0,1:T(8,128)(2,1)}, u32[]{:S(2)}) copy-start(bf16[256,64]{0,1:T(8,128)(2,1)} %param.11) | copy-start | bytes 98308
  212.9 45.6 %copy-start.3 = (bf16[256]{0:T(256)(128)(2,1)S(1)}, bf16[256]{0:T(256)(128)(2,1)}, u32[]{:S(2)}) copy-start(bf16[256]{0:T(256)(128)(2,1)} %param.10) | copy-start | bytes 1540

commit v3 on v2

v3 whole, which is shorter than its diff:
```python
import functools

import jax
import jax.numpy as jnp
from jax import lax
from jax.experimental import pallas as pl
from jax.experimental.pallas import tpu as pltpu
from jax.sharding import PartitionSpec as P

EPS = 1e-5
LANE = 128
ROW_BLOCK = 272
EXPERT_BATCH = 8
VMEM_BYTES = 60 * 1024 * 1024
F32 = jnp.float32
BF16 = jnp.bfloat16
MESH = pl.DeviceIdType.MESH


def cost(flops, nbytes):
    return pl.CostEstimate(flops=int(flops), bytes_accessed=int(nbytes), transcendentals=0)


def greet(peers):
    barrier = pltpu.get_barrier_semaphore()
    count = 0
    for peer in peers:
        pl.semaphore_signal(barrier, inc=1, device_id=peer, device_id_type=MESH)
        count += 1
    pl.semaphore_wait(barrier, count)


def onehot_pieces(pos_row, rows_hi):
    tokens = pos_row.shape[1]
    hi = jnp.floor(pos_row * (1.0 / LANE))
    lo = pos_row - hi * LANE
    hi_iota = lax.broadcasted_iota(jnp.int32, (rows_hi, tokens), 0).astype(F32)
    lo_iota = lax.broadcasted_iota(jnp.int32, (LANE, tokens), 0).astype(F32)
    return hi == hi_iota, lo == lo_iota


def route_rows(capacity, experts, choice_ref, tok_ref, seg_ref, pos_ref):
    top_k, tokens = choice_ref.shape
    rows_hi = tok_ref.shape[0]
    rows = rows_hi * LANE
    blk = 256
    e_iota = lax.broadcasted_iota(jnp.int32, (experts, tokens), 0)
    assigned = jnp.zeros((experts, tokens), F32)
    for k in range(top_k):
        assigned += jnp.where(choice_ref[k:k + 1, :] == e_iota, 1.0, 0.0)
    r_i = lax.broadcasted_iota(jnp.int32, (blk, blk), 0)
    c_i = lax.broadcasted_iota(jnp.int32, (blk, blk), 1)
    tri = jnp.where(r_i < c_i, 1.0, 0.0).astype(BF16)
    carry = jnp.zeros((experts, 1), F32)
    before = []
    for b in range(tokens // blk):
        part = assigned[:, b * blk:(b + 1) * blk]
        within = jnp.dot(part.astype(BF16), tri, preferred_element_type=F32)
        before.append(within + carry)
        carry = carry + jnp.sum(part, axis=1, keepdims=True)
    before = jnp.concatenate(before, axis=1)
    kept = jnp.broadcast_to(jnp.minimum(carry, float(capacity)), (experts, LANE))
    kept_hi = jnp.floor(kept * (1.0 / 16.0))
    kept_lo = kept - kept_hi * 16.0
    er = lax.broadcasted_iota(jnp.int32, (experts, experts), 0)
    ec = lax.broadcasted_iota(jnp.int32, (experts, experts), 1)
    low = jnp.where(ec < er, 1.0, 0.0).astype(BF16)
    start = 16.0 * jnp.dot(low, kept_hi.astype(BF16), preferred_element_type=F32)
    start = start + jnp.dot(low, kept_lo.astype(BF16), preferred_element_type=F32)
    end = start + kept
    fill = jnp.zeros((LANE - experts, LANE), F32)
    start_t = jnp.transpose(jnp.concatenate([start, fill], axis=0))
    end_t = jnp.transpose(jnp.concatenate([end, fill], axis=0))
    seg_ref[0:1, :] = start_t[0:1, :].astype(jnp.int32)
    lane = lax.broadcasted_iota(jnp.int32, (1, LANE), 1)
    seg_ref[1:2, :] = jnp.where(lane == experts - 1, rows, end_t[0:1, :].astype(jnp.int32))
    value = jnp.where(before < capacity, before + start[:, 0:1], float(rows))
    t_val = lax.broadcasted_iota(jnp.int32, (1, tokens), 1) + 1
    t_hi = (t_val // 16).astype(F32)
    t_lo = (t_val % 16).astype(F32)
    acc = jnp.zeros((rows_hi, 2 * LANE), F32)
    for k in range(top_k):
        hit = choice_ref[k:k + 1, :] == e_iota
        pos = jnp.sum(jnp.where(hit, value, 0.0), axis=0, keepdims=True)
        pos_ref[k:k + 1, :] = pos
        is_hi, is_lo = onehot_pieces(pos, rows_hi)
        left = jnp.where(is_hi, 1.0, 0.0).astype(BF16)
        right = jnp.concatenate([jnp.where(is_lo, t_hi, 0.0), jnp.where(is_lo, t_lo, 0.0)], axis=0).astype(BF16)
        acc += lax.dot_general(left, right, (((1,), (1,)), ((), ())), preferred_element_type=F32)
    tok_ref[...] = (16.0 * acc[:, :LANE] + acc[:, LANE:]).astype(jnp.int32) - 1


def square_rows(block):
    block = block * block
    lanes = block[:, :LANE]
    for j in range(1, block.shape[1] // LANE):
        lanes = lanes + block[:, j * LANE:(j + 1) * LANE]
    return jnp.sum(jnp.transpose(lanes), axis=0, keepdims=True)


def share_squares(squares, emb_size, send, recv):
    me = lax.axis_index('emb')
    copies = []
    for j in range(1, emb_size):
        copies.append(pltpu.make_async_remote_copy(
            src_ref=squares.at[emb_size - 1], dst_ref=squares.at[j - 1],
            send_sem=send.at[j - 1], recv_sem=recv.at[j - 1],
            device_id={'emb': lax.rem(me + j, emb_size)}, device_id_type=MESH))
        copies[-1].start()
    return copies


def inverse_rms(squares, emb_size, model_width):
    whole = squares[emb_size - 1]
    for j in range(emb_size - 1):
        whole = whole + squares[j]
    return lax.rsqrt(whole / model_width + EPS)


def prepare_kernel(capacity, emb_size, model_width, choice_ref, hid_ref, pre_ref, wr_ref,
                   tok_ref, seg_ref, pos_ref, b_ref, logit_ref, squares, send, recv):
    tokens, width = hid_ref.shape
    me = lax.axis_index('emb')
    greet({'emb': lax.rem(me + j, emb_size)} for j in range(1, emb_size))
    for i in range(tokens // LANE):
        squares[emb_size - 1, i:i + 1, :] = square_rows(hid_ref[i * LANE:(i + 1) * LANE, :].astype(F32))
    copies = share_squares(squares, emb_size, send, recv)
    route_rows(capacity, wr_ref.shape[1], choice_ref, tok_ref, seg_ref, pos_ref)
    for copy in copies:
        copy.wait_recv()
    inv = inverse_rms(squares, emb_size, model_width)
    pre = pre_ref[...].astype(F32)
    for i in range(tokens // LANE):
        col = jnp.concatenate([column_of(inv[i:i + 1, :])] * (width // LANE), axis=1)
        part = slice(i * LANE, (i + 1) * LANE)
        b_ref[part, :] = (hid_ref[part, :].astype(F32) * col * pre).astype(BF16)
    logit_ref[...] = lax.dot_general(wr_ref[...], b_ref[...], (((0,), (1,)), ((), ())), preferred_element_type=F32)
    for copy in copies:
        copy.wait_send()


def prepare(choice_t, hidden, norm_pre, w_router, capacity, emb_size):
    tokens, width = hidden.shape
    top_k = choice_t.shape[0]
    experts = w_router.shape[1]
    rows_hi = tokens * top_k // LANE
    dma = pltpu.SemaphoreType.DMA((emb_size - 1,))
    vmem = pl.BlockSpec(memory_space=pltpu.VMEM)
    return pl.pallas_call(
        functools.partial(prepare_kernel, capacity, emb_size, width * emb_size),
        out_shape=(
            jax.ShapeDtypeStruct((rows_hi, LANE), jnp.int32),
            jax.ShapeDtypeStruct((2, LANE), jnp.int32),
            jax.ShapeDtypeStruct((top_k, tokens), F32),
            jax.ShapeDtypeStruct((tokens, width), BF16),
            jax.ShapeDtypeStruct((experts, tokens), F32),
        ),
        in_specs=[vmem] * 4,
        out_specs=(vmem,) * 5,
        scratch_shapes=[pltpu.VMEM((emb_size, tokens // LANE, LANE), F32), dma, dma],
        compiler_params=pltpu.CompilerParams(collective_id=0, has_side_effects=True, vmem_limit_bytes=VMEM_BYTES),
        cost_estimate=cost(15e9, 4e6),
        name='prepare',
    )(choice_t, hidden, norm_pre.reshape(1, width), w_router)


def column_of(row):
    return jnp.transpose(jnp.broadcast_to(row, (LANE, LANE)))


def strips(tok, iota, count, axis):
    match = jnp.where(jnp.bitwise_and(tok, LANE - 1) == iota, 1.0, 0.0).astype(BF16)
    high = lax.shift_right_arithmetic(tok, 7).astype(F32).astype(BF16)
    zero = jnp.zeros_like(match)
    return jnp.concatenate([jnp.where(high == jnp.asarray(j, BF16), match, zero) for j in range(count)], axis=axis)


def grouped(seg_ref, step, in_ref, weights, out_ref):
    total = out_ref.shape[0]
    batch = len(weights)

    def block(e, w, offset):
        base = (seg_ref[0, e] // 16) * 16 + offset
        r0 = pl.multiple_of(jnp.minimum(base, total - ROW_BLOCK), 16)
        return r0, jnp.dot(in_ref[pl.ds(r0, ROW_BLOCK), :], w(), preferred_element_type=F32).astype(BF16)

    def put(r0, new, keep):
        row = r0 + lax.broadcasted_iota(jnp.int32, new.shape, 0)
        out_ref[pl.ds(r0, ROW_BLOCK), :] = jnp.where(keep(row), new, out_ref[pl.ds(r0, ROW_BLOCK), :])

    for q, (r0, new) in enumerate([block(step * batch + q, weights[q], 0) for q in range(batch)]):
        put(r0, new, lambda row: row >= seg_ref[0, step * batch + q])
    for q in range(batch):
        e = step * batch + q
        s, end = seg_ref[0, e], seg_ref[1, e]
        count = (end - (s // 16) * 16 + ROW_BLOCK - 1) // ROW_BLOCK

        def body(j, carry):
            r0, new = block(e, weights[q], j * ROW_BLOCK)
            put(r0, new, lambda row: jnp.logical_and(row >= s, row < end))
            return carry

        lax.fori_loop(1, count, body, 0)


def dispatch_up_kernel(steps, seg_ref, tok_ref, b_ref, wg_ref, wu_ref, z_ref, x_ref):
    i = pl.program_id(0)
    tokens = b_ref.shape[0]
    rows = x_ref.shape[0] // steps

    @pl.when(i < steps)
    def gather():
        lane = lax.broadcasted_iota(jnp.int32, (LANE, LANE), 1)
        pick = jnp.concatenate([
            strips(column_of(tok_ref[pl.ds(i * (rows // LANE) + q, 1), :]), lane, tokens // LANE, 1)
            for q in range(rows // LANE)], axis=0)
        at = pl.ds(pl.multiple_of(i * rows, rows), rows)
        x_ref[at, :] = jnp.dot(pick, b_ref[...], preferred_element_type=F32).astype(BF16)

    @pl.when(i >= steps)
    def project():
        pick = lambda q: lambda: jnp.concatenate([wg_ref[q], wu_ref[q]], axis=1)
        grouped(seg_ref, i - steps, x_ref, [pick(q) for q in range(wg_ref.shape[0])], z_ref)


def dispatch_up(seg, tok, b, w_gate, w_up):
    tokens, width = b.shape
    rows = tok.size
    experts, _, ffn = w_gate.shape
    steps = rows // 1024
    whole = lambda i, seg: (0, 0)
    one = pl.Buffered(1)
    w_spec = pl.BlockSpec((EXPERT_BATCH, width, ffn), lambda i, seg: (jnp.maximum(i - steps, 0), 0, 0))
    return pl.pallas_call(
        functools.partial(dispatch_up_kernel, steps),
        out_shape=jax.ShapeDtypeStruct((rows, 2 * ffn), BF16),
        grid_spec=pltpu.PrefetchScalarGridSpec(
            num_scalar_prefetch=1,
            grid=(steps + experts // EXPERT_BATCH,),
            in_specs=[pl.BlockSpec(tok.shape, whole, pipeline_mode=one), pl.BlockSpec(b.shape, whole, pipeline_mode=one), w_spec, w_spec],
            out_specs=pl.BlockSpec((rows, 2 * ffn), whole, pipeline_mode=one),
            scratch_shapes=[pltpu.VMEM((rows, width), BF16)],
        ),
        compiler_params=pltpu.CompilerParams(vmem_limit_bytes=VMEM_BYTES),
        cost_estimate=cost(2 * rows * width * (tokens + 2 * ffn), 8 * rows * width),
        name='dispatch_up',
    )(seg, tok, b, w_gate, w_up)


def exchange_kernel(emb_size, subs, z_ref, logit_ref, choice_ref, pos_ref, g_ref, gate_ref,
                    mine, theirs, ring, got, gates, load, send_p, recv_p, send_r, recv_r,
                    send_a, recv_a, send_d, recv_d, send_l, recv_l, send_g, recv_g):
    chips = emb_size // 2
    last = chips - 1
    me = lax.axis_index('emb')
    chip, core = me // 2, lax.rem(me, 2)
    partner = {'emb': chip * 2 + 1 - core}
    ways = [{'emb': lax.rem(me + 2, emb_size)}, {'emb': lax.rem(me + emb_size - 2, emb_size)}]
    own = z_ref.shape[0] // emb_size
    half = own // 2
    sub = half // subs
    ffn = g_ref.shape[1]
    greet({'emb': lax.rem(me + j, emb_size)} for j in range(1, emb_size))

    def around(c):
        return lax.rem(c + 2 * chips, chips)

    def target(d, step):
        return around(chip - 1 - step if d == 0 else chip + 1 + step)

    def rows(c, parity, d, u, size):
        return pl.ds(pl.multiple_of((c * 2 + parity) * own + d * half + u * sub, sub), size)

    order = [(step, u, d) for step in range(chips) for u in range(subs) for d in range(2)]
    loads, passed, sums = {}, {}, {}
    for step, u, d in order:
        c = target(d, step)
        copy = pltpu.make_async_remote_copy(
            src_ref=z_ref.at[rows(c, 1 - core, d, u, sub), :], dst_ref=theirs.at[step, d, u],
            send_sem=send_p.at[step, d, u], recv_sem=recv_p.at[step, d, u],
            device_id=partner, device_id_type=MESH)
        copy.start()
        passed[step, d, u] = copy
        copy = pltpu.make_async_copy(z_ref.at[rows(c, core, d, u, sub), :], mine.at[step, d, u], load.at[step, d, u])
        copy.start()
        loads[step, d, u] = copy

    experts, tokens = logit_ref.shape
    share_tok = tokens // emb_size

    def columns(who):
        return pl.ds(pl.multiple_of(who * share_tok, share_tok), share_tok)

    parts, picked = [], []
    for j in range(1, emb_size):
        peer = lax.rem(me + j, emb_size)
        parts.append(pltpu.make_async_remote_copy(
            src_ref=logit_ref.at[:, columns(peer)], dst_ref=got.at[j - 1],
            send_sem=send_l.at[j - 1], recv_sem=recv_l.at[j - 1],
            device_id={'emb': peer}, device_id_type=MESH))
        parts[-1].start()

    def pick_gates():
        logits = logit_ref[:, columns(me)]
        for j in range(1, emb_size):
            parts[j - 1].wait_recv()
            logits = logits + got[j - 1]
        grown = jnp.exp(logits - jnp.max(logits, axis=0, keepdims=True))
        prob = grown / jnp.sum(grown, axis=0, keepdims=True)
        e_iota = lax.broadcasted_iota(jnp.int32, (experts, share_tok), 0)
        chosen = choice_ref[:, columns(me)]
        for k in range(chosen.shape[0]):
            gate = jnp.sum(jnp.where(chosen[k:k + 1, :] == e_iota, prob, 0.0), axis=0, keepdims=True)
            gates[k:k + 1, columns(me)] = gate
        for j in range(1, emb_size):
            picked.append(pltpu.make_async_remote_copy(
                src_ref=gates.at[:, columns(me)], dst_ref=gates.at[:, columns(me)],
                send_sem=send_g.at[j - 1], recv_sem=recv_g.at[j - 1],
                device_id={'emb': lax.rem(me + j, emb_size)}, device_id_type=MESH))
            picked[-1].start()

    spread = {}

    def scatter(d, way, step, c, u):
        at = rows(c, core, d, u, sub)
        copy = pltpu.make_async_remote_copy(
            src_ref=g_ref.at[at, :], dst_ref=g_ref.at[at, :],
            send_sem=send_a.at[way, step, d, u], recv_sem=recv_a.at[way, step, d, u],
            device_id=ways[way], device_id_type=MESH)
        copy.start()
        spread[way, step, d, u] = copy

    across = {}

    def share(d, slot, c, u):
        at = rows(c, core, d, u, sub)
        copy = pltpu.make_async_remote_copy(
            src_ref=g_ref.at[at, :], dst_ref=g_ref.at[at, :],
            send_sem=send_d.at[slot, d, u], recv_sem=recv_d.at[slot, d, u],
            device_id=partner, device_id_type=MESH)
        copy.start()
        across[slot, d, u] = copy

    def sends(way, step, d):
        if step < (chips - 1) // 2:
            return True
        return step == (chips - 1) // 2 and chips % 2 == 0 and way == d

    piece = 32
    for step, u, d in order:
        if (u, d) == (0, 0) and step == 1:
            pick_gates()
        if (u, d) == (0, 0) and step == min(2, last):
            for copy in picked:
                copy.wait_recv()
            place_gates(pos_ref, gates, gate_ref)
        loads[step, d, u].wait()
        passed[step, d, u].wait_recv()
        if step >= 1:
            sums[step - 1, d, u].wait_recv()
        if step < last:
            def add(i, carry):
                at = pl.ds(pl.multiple_of(i * piece, piece), piece)
                v = mine[step, d, u, at, :].astype(F32) + theirs[step, d, u, at, :].astype(F32)
                if step >= 1:
                    v = v + ring[step - 1, d, u, at, :].astype(F32)
                mine[step, d, u, at, :] = v.astype(BF16)
                return carry

            lax.fori_loop(0, sub // piece, add, 0)
            copy = pltpu.make_async_remote_copy(
                src_ref=mine.at[step, d, u], dst_ref=ring.at[step, d, u],
                send_sem=send_r.at[step, d, u], recv_sem=recv_r.at[step, d, u],
                device_id=ways[d], device_id_type=MESH)
            copy.start()
            sums[step, d, u] = copy
        else:
            def act(i, carry):
                at = pl.ds(pl.multiple_of(i * piece, piece), piece)
                v = mine[step, d, u, at, :].astype(F32) + theirs[step, d, u, at, :].astype(F32)
                v = (v + ring[step - 1, d, u, at, :].astype(F32)).astype(BF16).astype(F32)
                v = jax.nn.gelu(v[:, :ffn], approximate=True) * v[:, ffn:]
                out = pl.ds(pl.multiple_of((chip * 2 + core) * own + d * half + u * sub + i * piece, piece), piece)
                g_ref[out, :] = v.astype(BF16)
                return carry

            lax.fori_loop(0, sub // piece, act, 0)
            for way in range(2):
                if sends(way, 0, d):
                    scatter(d, way, 0, chip, u)
            share(d, 0, chip, u)
    slot = 0
    for step in range(chips // 2):
        for u in range(subs):
            for way in range(2):
                for d in range(2):
                    if sends(way, step, d):
                        spread[way, step, d, u].wait_recv()
                        c = around(chip - 1 - step if way == 0 else chip + 1 + step)
                        if sends(way, step + 1, d):
                            scatter(d, way, step + 1, c, u)
                        full = sends(0, step, d) and sends(1, step, d)
                        share(d, 1 + 2 * step + (way if full else 0), c, u)
    for copy in across.values():
        copy.wait_recv()
    for group in (passed, sums, spread, across):
        for copy in group.values():
            copy.wait_send()
    for copy in parts + picked:
        copy.wait_send()


def exchange(z, logits, choice_t, pos, emb_size):
    rows, both = z.shape
    experts, tokens = logits.shape
    vmem = pl.BlockSpec(memory_space=pltpu.VMEM)
    peers = pltpu.SemaphoreType.DMA((emb_size - 1,))
    chips = emb_size // 2
    own = rows // emb_size
    subs = 4
    sub = own // (2 * subs)
    dma = pltpu.SemaphoreType.DMA
    part = (chips, 2, subs)
    hop = (chips - 1, 2, subs)
    fan = (2, max(chips // 2, 1), 2, subs)
    return pl.pallas_call(
        functools.partial(exchange_kernel, emb_size, subs),
        out_shape=(jax.ShapeDtypeStruct((rows, both // 2), BF16), jax.ShapeDtypeStruct((rows // LANE, LANE), F32)),
        in_specs=[pl.BlockSpec(memory_space=pl.ANY), vmem, vmem, vmem],
        out_specs=(vmem, vmem),
        scratch_shapes=[
            pltpu.VMEM(part + (sub, both), BF16),
            pltpu.VMEM(part + (sub, both), BF16),
            pltpu.VMEM(hop + (sub, both), BF16),
            pltpu.VMEM((emb_size - 1, experts, tokens // emb_size), F32),
            pltpu.VMEM(choice_t.shape, F32),
            dma(part), dma(part), dma(part), dma(hop), dma(hop), dma(fan), dma(fan), dma(part), dma(part),
            peers, peers, peers, peers,
        ],
        compiler_params=pltpu.CompilerParams(collective_id=2, has_side_effects=True, vmem_limit_bytes=VMEM_BYTES),
        cost_estimate=cost(100e9, 4 * rows * both),
        name='exchange',
    )(z, logits, choice_t, pos)


def place_gates(pos_ref, gates, gate_ref):
    top_k = pos_ref.shape[0]
    rows_hi = gate_ref.shape[0]
    acc = jnp.zeros((rows_hi, 3 * LANE), F32)
    for k in range(top_k):
        is_hi, is_lo = onehot_pieces(pos_ref[k:k + 1, :], rows_hi)
        left = jnp.where(is_hi, 1.0, 0.0).astype(BF16)
        pieces = []
        rest = gates[k:k + 1, :]
        for _ in range(3):
            piece = rest.astype(BF16).astype(F32)
            rest = rest - piece
            pieces.append(jnp.where(is_lo, piece, 0.0).astype(BF16))
        right = jnp.concatenate(pieces, axis=0)
        acc += lax.dot_general(left, right, (((1,), (1,)), ((), ())), preferred_element_type=F32)
    gate_ref[...] = acc[:, :LANE] + acc[:, LANE:2 * LANE] + acc[:, 2 * LANE:]


def finish_kernel(ffn_size, emb_size, model_width, u_ref, tok_ref, hid_ref, post_ref, out_ref, rows_u, part, got,
                  total, squares, load, send_a, recv_a, send_b, recv_b, send_c, recv_c):
    tokens, width = out_ref.shape
    own = tokens // ffn_size
    half = own // 2
    subs = got.shape[2]
    sub = half // subs
    last = ffn_size - 1
    me = lax.axis_index('ffn')
    emb = lax.axis_index('emb')
    peers = [{'ffn': lax.rem(me + 1, ffn_size)}, {'ffn': lax.rem(me + ffn_size - 1, ffn_size)}]
    blocks = load.shape[0]
    size = rows_u.shape[0] // blocks

    def fetch(i):
        at = pl.ds(pl.multiple_of(i * size, size), size)
        return pltpu.make_async_copy(u_ref.at[at, :], rows_u.at[at, :], load.at[i])

    for i in range(blocks):
        fetch(i).start()
    greet(peers + [{'emb': lax.rem(emb + j, emb_size)} for j in range(1, emb_size)])
    t_iota = lax.broadcasted_iota(jnp.int32, (half, LANE), 0)

    def combine(d, step):
        chunk = me - 1 - step if d == 0 else me + 1 + step
        first = lax.rem(chunk + ffn_size * 2, ffn_size) * own + d * half
        part[d, step] = jnp.zeros((half, width), F32)

        def body(i, carry):
            if (d, step) == (0, 0):
                fetch(i).wait()
            pick = jnp.concatenate([
                jnp.where(tok_ref[pl.ds(i * (size // LANE) + q, 1), :] - first == t_iota, 1.0, 0.0).astype(BF16)
                for q in range(size // LANE)], axis=1)
            at = pl.ds(pl.multiple_of(i * size, size), size)
            part[d, step] = part[d, step] + jnp.dot(pick, rows_u[at, :], preferred_element_type=F32)
            return carry

        lax.fori_loop(0, blocks, body, 0)

    sums = {}
    for step in range(ffn_size):
        for d in range(2):
            combine(d, step)
        for u in range(subs):
            for d in range(2):
                at = pl.ds(u * sub, sub)
                if step >= 1:
                    sums[d, step - 1, u].wait_recv()
                    value = got[d, step - 1, u] + part[d, step, at, :]
                    if step == last:
                        total[d * half + u * sub:d * half + (u + 1) * sub, :] = value
                    else:
                        got[d, step - 1, u] = value
                if step < last:
                    copy = pltpu.make_async_remote_copy(
                        src_ref=part.at[d, 0, at, :] if step == 0 else got.at[d, step - 1, u], dst_ref=got.at[d, step, u],
                        send_sem=send_a.at[d, step, u], recv_sem=recv_a.at[d, step, u],
                        device_id=peers[d], device_id_type=MESH)
                    copy.start()
                    sums[d, step, u] = copy
    for i in range(own // LANE):
        squares[emb_size - 1, i:i + 1, :] = square_rows(total[i * LANE:(i + 1) * LANE, :])
    shares = share_squares(squares, emb_size, send_b, recv_b)
    for copy in shares:
        copy.wait_recv()
    inv = inverse_rms(squares, emb_size, model_width)
    post = post_ref[...].astype(F32)

    def rows(chunk, start, size):
        chunk = lax.rem(chunk + ffn_size * 2, ffn_size)
        return pl.ds(pl.multiple_of(chunk * own + start, size), size)

    for i in range(own // LANE):
        col = jnp.concatenate([column_of(inv[i:i + 1, :])] * (width // LANE), axis=1)
        at = rows(me, i * LANE, LANE)
        out_ref[at, :] = (hid_ref[at, :].astype(F32) + total[i * LANE:(i + 1) * LANE, :] * col * post).astype(BF16)
    spread = []
    for step in range(ffn_size // 2):
        if step >= 1:
            for copy in spread[-2:]:
                copy.wait_recv()
        last = step == (ffn_size - 1) // 2
        for d in range(2):
            chunk = me - step if d == 0 else me + step
            at = rows(chunk, d * own // 2, own // 2) if last else rows(chunk, 0, own)
            spread.append(pltpu.make_async_remote_copy(
                src_ref=out_ref.at[at, :], dst_ref=out_ref.at[at, :],
                send_sem=send_c.at[d, step], recv_sem=recv_c.at[d, step],
                device_id=peers[d], device_id_type=MESH))
            spread[-1].start()
    for copy in spread[-2:]:
        copy.wait_recv()
    for copy in list(sums.values()) + shares + spread:
        copy.wait_send()


def finish(u, tok, hidden, norm_post, ffn_size, emb_size):
    tokens, width = hidden.shape
    rows = u.shape[0]
    own = tokens // ffn_size
    half = own // 2
    subs = 2 if half % 256 == 0 else 1
    vmem = pl.BlockSpec(memory_space=pltpu.VMEM)
    dma = pltpu.SemaphoreType.DMA
    hops = (2, ffn_size - 1, subs)
    return pl.pallas_call(
        functools.partial(finish_kernel, ffn_size, emb_size, width * emb_size),
        out_shape=jax.ShapeDtypeStruct((tokens, width), BF16),
        in_specs=[pl.BlockSpec(memory_space=pl.ANY), vmem, vmem, vmem],
        out_specs=vmem,
        scratch_shapes=[
            pltpu.VMEM((rows, width), BF16),
            pltpu.VMEM((2, ffn_size, half, width), F32),
            pltpu.VMEM(hops + (half // subs, width), F32),
            pltpu.VMEM((own, width), F32),
            pltpu.VMEM((emb_size, own // LANE, LANE), F32),
            dma((rows // 2048,)), dma(hops), dma(hops),
            dma((emb_size - 1,)), dma((emb_size - 1,)),
            dma((2, ffn_size // 2)), dma((2, ffn_size // 2)),
        ],
        compiler_params=pltpu.CompilerParams(collective_id=1, has_side_effects=True, vmem_limit_bytes=VMEM_BYTES),
        cost_estimate=cost(2 * rows * tokens * width, 16e6),
        name='finish',
    )(u, tok, hidden, norm_post.reshape(1, width))


def down_kernel(seg_ref, gate_ref, g_ref, w_ref, u_ref):
    width = u_ref.shape[1]
    pick = lambda q: lambda: w_ref[q]
    grouped(seg_ref, pl.program_id(0), g_ref, [pick(q) for q in range(w_ref.shape[0])], u_ref)

    @pl.when(pl.program_id(0) == pl.num_programs(0) - 1)
    def scale():
        def body(i, carry):
            for q in range(4):
                hi = i * 4 + q
                col = jnp.concatenate([column_of(gate_ref[pl.ds(hi, 1), :])] * (width // LANE), axis=1)
                at = pl.ds(pl.multiple_of(hi * LANE, LANE), LANE)
                u_ref[at, :] = (u_ref[at, :].astype(F32) * col).astype(BF16)
            return carry

        lax.fori_loop(0, gate_ref.shape[0] // 4, body, 0)


def expert_down(seg, gate, act, w_down):
    rows, ffn = act.shape
    experts, _, width = w_down.shape
    whole = lambda e, seg: (0, 0)
    one = pl.Buffered(1)
    return pl.pallas_call(
        down_kernel,
        out_shape=jax.ShapeDtypeStruct((rows, width), BF16),
        grid_spec=pltpu.PrefetchScalarGridSpec(
            num_scalar_prefetch=1,
            grid=(experts // EXPERT_BATCH,),
            in_specs=[
                pl.BlockSpec(gate.shape, whole, pipeline_mode=one),
                pl.BlockSpec(act.shape, whole, pipeline_mode=one),
                pl.BlockSpec((EXPERT_BATCH, ffn, width), lambda e, seg: (e, 0, 0)),
            ],
            out_specs=pl.BlockSpec((rows, width), whole, pipeline_mode=one),
        ),
        compiler_params=pltpu.CompilerParams(vmem_limit_bytes=VMEM_BYTES),
        cost_estimate=cost(2 * rows * width * ffn, 4 * rows * width),
        name='expert_down',
    )(seg, gate, act, w_down)


def solution(mesh):
    emb_size = mesh.shape['emb']
    ffn_size = mesh.shape['ffn']

    def local_block(hidden, norm_pre, norm_post, w_router, w_gate, w_up, w_down, choice):
        num_tok, local_width = hidden.shape
        experts = w_gate.shape[0]
        top_k = choice.shape[1]
        capacity = 2 * num_tok * top_k // experts
        choice_t = choice.T
        tok, seg, pos, normed, logits = prepare(choice_t, hidden, norm_pre, w_router, capacity, emb_size)
        z = dispatch_up(seg, tok, normed, w_gate, w_up)
        act, gate = exchange(z, logits, choice_t, pos, emb_size)
        u = expert_down(seg, gate, act, w_down)
        return finish(u, tok, hidden, norm_post, ffn_size, emb_size)

    in_specs = (P('dp', 'emb'), P('emb'), P('emb'), P('emb', None), P(None, 'emb', 'ffn'), P(None, 'emb', 'ffn'), P(None, 'ffn', 'emb'), P('dp', None))
    return jax.shard_map(local_block, mesh=mesh, in_specs=in_specs, out_specs=P('dp', 'emb'), check_vma=False)
```

time: 306 us -> 256 us (0.84)
  Pallas kernels: 285 us -> 249 us
  blocking collectives: 14.1 us -> 0 us
    pallas_call x6 -> x3, Pallas kernels: 128 us -> 75.5 us  [the longest x1 41.1 us: dispatch_up(): pl.pallas_call(functools.partial(dispatch_up_kernel, steps), out_shape=ja...]
    psum x1 -> x0, blocking collectives: 14.1 us -> none  [local_block(): sq_pre = lax.psum(jnp.sum(hid_f32 * hid_f32, axis=1), 'emb')]
    pallas_call x1, Pallas kernels: 43 us -> 52.8 us  [finish(): pl.pallas_call(functools.partial(finish_kernel, ffn_size, emb_size, width...]
    pallas_call x1, Pallas kernels: 114 us -> 121 us  [exchange(): pl.pallas_call(functools.partial(exchange_kernel, emb_size, subs), out_sh...]
where the time goes in v3:
time: 256 us; the launch traced here: 255 us
  Pallas kernels  249 us (97%)
  local copies, waits for them, and re-layouts  5.57 us (2%)
    pallas_call x1, Pallas kernels, exchange(): pl.pallas_call(functools.partial(exchange_kernel, emb_size, subs), out_sh...  121 us
    pallas_call x1, Pallas kernels, finish(): pl.pallas_call(functools.partial(finish_kernel, ffn_size, emb_size, width...  52.8 us
    pallas_call x1, Pallas kernels, dispatch_up(): pl.pallas_call(functools.partial(dispatch_up_kernel, steps), out_shape=ja...  41.1 us
    pallas_call x1, Pallas kernels, expert_down(): pl.pallas_call(down_kernel, out_shape=jax.ShapeDtypeStruct((rows, width),...  21.4 us
    pallas_call x1, Pallas kernels, prepare(): pl.pallas_call(functools.partial(prepare_kernel, capacity, emb_size, widt...  13.1 us

profile of v3, /device:TPU:97, one launch (start us, length us, event | category | flops | bytes accessed | tf_op | source)
XLA Modules:
  0.0 254.8 jit_solution(2703964419205888762)
XLA Ops:
  0.0 1.5 copy.9.wr_ref
  1.5 1.2 reshape.6.pre_ref
  2.7 13.1 %prepare.1 = (s32[128,128]{1,0:T(8,128)}, s32[2,128]{1,0:T(2,128)}, f32[8,2048]{1,0:T(8,128)}, bf16[2048,256]{1,0:T(8,128)(2,1)}, f32[64,2048]{1,0:T(8,128)}) custom-call(s32[8,2048]{1,0:T(8,128)} %bitcast.1, bf16[2048,256]{1,0:T(8,128)(2,1)} %hid_ref.3, bf16[1,256]{1,0:T(2,128)(2,1)} %reshape.6.pre_ref, bf16[256,64]{1,0:T(8,128)(2,1)} %copy.9.wr_ref), custom_call_target="tpu_custom_call" | custom-call | flops 15000000512 | bytes 4000000 | tf_op jit(solution)/shard_map/prepare/pallas_call | solution.py:149
  15.8 41.1 %dispatch_up.1.z_ref = bf16[16384,512]{1,0:T(8,128)(2,1)} custom-call(s32[2,128]{1,0:T(2,128)} %get-tuple-element.12.seg_ref, s32[128,128]{1,0:T(8,128)} %get-tuple-element.13.tok_ref, bf16[2048,256]{1,0:T(8,128)(2,1)} %get-tuple-element.14.b_ref, bf16[64,256,256]{2,1,0:T(8,128)(2,1)} %wg_ref.1, bf16[64,256,256]{2,1,0:T(8,128)(2,1)} %wu_ref.1), custom_call_target="tpu_custom_call" | custom-call | flops 21474836480 | bytes 33554432 | tf_op jit(solution)/shard_map/dispatch_up/pallas_call | solution.py:234
  56.9 120.8 %exchange.1 = (bf16[16384,256]{1,0:T(8,128)(2,1)}, f32[128,128]{1,0:T(8,128)}) custom-call(bf16[16384,512]{1,0:T(8,128)(2,1)} %dispatch_up.1.z_ref, f32[64,2048]{1,0:T(8,128)} %get-tuple-element.15.logit_ref, s32[8,2048]{1,0:T(8,128)} %bitcast.2, f32[8,2048]{1,0:T(8,128)} %get-tuple-element.16.pos_ref), custom_call_target="tpu_custom_call" | custom-call | flops 99999997952 | bytes 33554432 | tf_op jit(solution)/shard_map/exchange/pallas_call | solution.py:426
  177.7 0.0 copy-start
  177.8 21.4 %expert_down.1.u_ref = bf16[16384,256]{1,0:T(8,128)(2,1)} custom-call(s32[2,128]{1,0:T(2,128)} %get-tuple-element.12.seg_ref, f32[128,128]{1,0:T(8,128)} %get-tuple-element.17.gate_ref, bf16[16384,256]{1,0:T(8,128)(2,1)} %get-tuple-element.18.g_ref, bf16[64,256,256]{2,1,0:T(8,128)(2,1)} %w_ref.1), custom_call_target="tpu_custom_call" | custom-call | flops 2147483648 | bytes 16777216 | tf_op jit(solution)/shard_map/expert_down/pallas_call | solution.py:614
  199.1 0.0 copy-done
  199.1 0.6 reshape.7.post_ref
  199.7 52.8 %finish.1 = bf16[2048,256]{1,0:T(8,128)(2,1)} custom-call(bf16[16384,256]{1,0:T(8,128)(2,1)} %expert_down.1.u_ref, s32[128,128]{1,0:T(8,128)} %get-tuple-element.13.tok_ref, bf16[2048,256]{1,0:T(8,128)(2,1)} %hid_ref.3, bf16[1,256]{1,0:T(2,128)(2,1)} %reshape.7.post_ref), custom_call_target="tpu_custom_call" | custom-call | flops 17179869184 | bytes 16000000 | tf_op jit(solution)/shard_map/finish/pallas_call | solution.py:570
  252.5 2.3 copy.11
Async XLA Ops:
  177.7 21.4 %copy-start = (bf16[256]{0:T(256)(128)(2,1)S(1)}, bf16[256]{0:T(256)(128)(2,1)}, u32[]{:S(2)}) copy-start(bf16[256]{0:T(256)(128)(2,1)} %param.10) | copy-start | bytes 1540

commit v4 on v3

--- a/solution.py
+++ b/solution.py
@@ -125,16 +125,16 @@
     for i in range(tokens // LANE):
         squares[emb_size - 1, i:i + 1, :] = square_rows(hid_ref[i * LANE:(i + 1) * LANE, :].astype(F32))
     copies = share_squares(squares, emb_size, send, recv)
-    route_rows(capacity, wr_ref.shape[1], choice_ref, tok_ref, seg_ref, pos_ref)
+    route_rows(capacity, wr_ref.shape[0], choice_ref, tok_ref, seg_ref, pos_ref)
     for copy in copies:
         copy.wait_recv()
     inv = inverse_rms(squares, emb_size, model_width)
-    pre = pre_ref[...].astype(F32)
+    pre = pre_ref[...].reshape(1, width).astype(F32)
     for i in range(tokens // LANE):
         col = jnp.concatenate([column_of(inv[i:i + 1, :])] * (width // LANE), axis=1)
         part = slice(i * LANE, (i + 1) * LANE)
         b_ref[part, :] = (hid_ref[part, :].astype(F32) * col * pre).astype(BF16)
-    logit_ref[...] = lax.dot_general(wr_ref[...], b_ref[...], (((0,), (1,)), ((), ())), preferred_element_type=F32)
+    logit_ref[...] = lax.dot_general(wr_ref[...], b_ref[...], (((1,), (1,)), ((), ())), preferred_element_type=F32)
     for copy in copies:
         copy.wait_send()
 
@@ -161,7 +161,7 @@
         compiler_params=pltpu.CompilerParams(collective_id=0, has_side_effects=True, vmem_limit_bytes=VMEM_BYTES),
         cost_estimate=cost(15e9, 4e6),
         name='prepare',
-    )(choice_t, hidden, norm_pre.reshape(1, width), w_router)
+    )(choice_t, hidden, norm_pre, w_router.T)
 
 
 def column_of(row):
@@ -176,20 +176,19 @@
 
 
 def grouped(seg_ref, step, in_ref, weights, out_ref):
-    total = out_ref.shape[0]
     batch = len(weights)
 
     def block(e, w, offset):
-        base = (seg_ref[0, e] // 16) * 16 + offset
-        r0 = pl.multiple_of(jnp.minimum(base, total - ROW_BLOCK), 16)
+        r0 = pl.multiple_of((seg_ref[0, e] // 16) * 16 + offset, 16)
         return r0, jnp.dot(in_ref[pl.ds(r0, ROW_BLOCK), :], w(), preferred_element_type=F32).astype(BF16)
 
-    def put(r0, new, keep):
-        row = r0 + lax.broadcasted_iota(jnp.int32, new.shape, 0)
-        out_ref[pl.ds(r0, ROW_BLOCK), :] = jnp.where(keep(row), new, out_ref[pl.ds(r0, ROW_BLOCK), :])
-
-    for q, (r0, new) in enumerate([block(step * batch + q, weights[q], 0) for q in range(batch)]):
-        put(r0, new, lambda row: row >= seg_ref[0, step * batch + q])
+    for q in range(batch):
+        e = step * batch + q
+        r0, new = block(e, weights[q], 0)
+        head = out_ref[pl.ds(r0, 16), :]
+        row = r0 + lax.broadcasted_iota(jnp.int32, head.shape, 0)
+        out_ref[pl.ds(r0, 16), :] = jnp.where(row >= seg_ref[0, e], new[:16, :], head)
+        out_ref[pl.ds(r0 + 16, ROW_BLOCK - 16), :] = new[16:, :]
     for q in range(batch):
         e = step * batch + q
         s, end = seg_ref[0, e], seg_ref[1, e]
@@ -197,7 +196,9 @@
 
         def body(j, carry):
             r0, new = block(e, weights[q], j * ROW_BLOCK)
-            put(r0, new, lambda row: jnp.logical_and(row >= s, row < end))
+            row = r0 + lax.broadcasted_iota(jnp.int32, new.shape, 0)
+            keep = jnp.logical_and(row >= s, row < end)
+            out_ref[pl.ds(r0, ROW_BLOCK), :] = jnp.where(keep, new, out_ref[pl.ds(r0, ROW_BLOCK), :])
             return carry
 
         lax.fori_loop(1, count, body, 0)
@@ -206,7 +207,7 @@
 def dispatch_up_kernel(steps, seg_ref, tok_ref, b_ref, wg_ref, wu_ref, z_ref, x_ref):
     i = pl.program_id(0)
     tokens = b_ref.shape[0]
-    rows = x_ref.shape[0] // steps
+    rows = (x_ref.shape[0] - ROW_BLOCK) // steps
 
     @pl.when(i < steps)
     def gather():
@@ -233,13 +234,13 @@
     w_spec = pl.BlockSpec((EXPERT_BATCH, width, ffn), lambda i, seg: (jnp.maximum(i - steps, 0), 0, 0))
     return pl.pallas_call(
         functools.partial(dispatch_up_kernel, steps),
-        out_shape=jax.ShapeDtypeStruct((rows, 2 * ffn), BF16),
+        out_shape=jax.ShapeDtypeStruct((rows + ROW_BLOCK, 2 * ffn), BF16),
         grid_spec=pltpu.PrefetchScalarGridSpec(
             num_scalar_prefetch=1,
             grid=(steps + experts // EXPERT_BATCH,),
             in_specs=[pl.BlockSpec(tok.shape, whole, pipeline_mode=one), pl.BlockSpec(b.shape, whole, pipeline_mode=one), w_spec, w_spec],
-            out_specs=pl.BlockSpec((rows, 2 * ffn), whole, pipeline_mode=one),
-            scratch_shapes=[pltpu.VMEM((rows, width), BF16)],
+            out_specs=pl.BlockSpec((rows + ROW_BLOCK, 2 * ffn), whole, pipeline_mode=one),
+            scratch_shapes=[pltpu.VMEM((rows + ROW_BLOCK, width), BF16)],
         ),
         compiler_params=pltpu.CompilerParams(vmem_limit_bytes=VMEM_BYTES),
         cost_estimate=cost(2 * rows * width * (tokens + 2 * ffn), 8 * rows * width),
@@ -256,7 +257,7 @@
     chip, core = me // 2, lax.rem(me, 2)
     partner = {'emb': chip * 2 + 1 - core}
     ways = [{'emb': lax.rem(me + 2, emb_size)}, {'emb': lax.rem(me + emb_size - 2, emb_size)}]
-    own = z_ref.shape[0] // emb_size
+    own = gate_ref.size // emb_size
     half = own // 2
     sub = half // subs
     ffn = g_ref.shape[1]
@@ -411,7 +412,7 @@
 
 
 def exchange(z, logits, choice_t, pos, emb_size):
-    rows, both = z.shape
+    rows, both = choice_t.size, z.shape[1]
     experts, tokens = logits.shape
     vmem = pl.BlockSpec(memory_space=pltpu.VMEM)
     peers = pltpu.SemaphoreType.DMA((emb_size - 1,))
@@ -425,7 +426,7 @@
     fan = (2, max(chips // 2, 1), 2, subs)
     return pl.pallas_call(
         functools.partial(exchange_kernel, emb_size, subs),
-        out_shape=(jax.ShapeDtypeStruct((rows, both // 2), BF16), jax.ShapeDtypeStruct((rows // LANE, LANE), F32)),
+        out_shape=(jax.ShapeDtypeStruct((rows + ROW_BLOCK, both // 2), BF16), jax.ShapeDtypeStruct((rows // LANE, LANE), F32)),
         in_specs=[pl.BlockSpec(memory_space=pl.ANY), vmem, vmem, vmem],
         out_specs=(vmem, vmem),
         scratch_shapes=[
@@ -484,27 +485,31 @@
     greet(peers + [{'emb': lax.rem(emb + j, emb_size)} for j in range(1, emb_size)])
     t_iota = lax.broadcasted_iota(jnp.int32, (half, LANE), 0)
 
-    def combine(d, step):
-        chunk = me - 1 - step if d == 0 else me + 1 + step
-        first = lax.rem(chunk + ffn_size * 2, ffn_size) * own + d * half
-        part[d, step] = jnp.zeros((half, width), F32)
+    def combine(step):
+        firsts = []
+        for d in range(2):
+            chunk = me - 1 - step if d == 0 else me + 1 + step
+            firsts.append(lax.rem(chunk + ffn_size * 2, ffn_size) * own + d * half)
+            part[d, step] = jnp.zeros((half, width), F32)
 
         def body(i, carry):
-            if (d, step) == (0, 0):
+            if step == 0:
                 fetch(i).wait()
+            tok = [tok_ref[pl.ds(i * (size // LANE) + q, 1), :] for q in range(size // LANE)]
             pick = jnp.concatenate([
-                jnp.where(tok_ref[pl.ds(i * (size // LANE) + q, 1), :] - first == t_iota, 1.0, 0.0).astype(BF16)
-                for q in range(size // LANE)], axis=1)
+                jnp.concatenate([jnp.where(row - first == t_iota, 1.0, 0.0).astype(BF16) for row in tok], axis=1)
+                for first in firsts], axis=0)
             at = pl.ds(pl.multiple_of(i * size, size), size)
-            part[d, step] = part[d, step] + jnp.dot(pick, rows_u[at, :], preferred_element_type=F32)
+            value = jnp.dot(pick, rows_u[at, :], preferred_element_type=F32)
+            for d in range(2):
+                part[d, step] = part[d, step] + value[d * half:(d + 1) * half, :]
             return carry
 
         lax.fori_loop(0, blocks, body, 0)
 
     sums = {}
     for step in range(ffn_size):
-        for d in range(2):
-            combine(d, step)
+        combine(step)
         for u in range(subs):
             for d in range(2):
                 at = pl.ds(u * sub, sub)
@@ -528,7 +533,7 @@
     for copy in shares:
         copy.wait_recv()
     inv = inverse_rms(squares, emb_size, model_width)
-    post = post_ref[...].astype(F32)
+    post = post_ref[...].reshape(1, width).astype(F32)
 
     def rows(chunk, start, size):
         chunk = lax.rem(chunk + ffn_size * 2, ffn_size)
@@ -560,7 +565,7 @@
 
 def finish(u, tok, hidden, norm_post, ffn_size, emb_size):
     tokens, width = hidden.shape
-    rows = u.shape[0]
+    rows = tok.size
     own = tokens // ffn_size
     half = own // 2
     subs = 2 if half % 256 == 0 else 1
@@ -585,7 +590,7 @@
         compiler_params=pltpu.CompilerParams(collective_id=1, has_side_effects=True, vmem_limit_bytes=VMEM_BYTES),
         cost_estimate=cost(2 * rows * tokens * width, 16e6),
         name='finish',
-    )(u, tok, hidden, norm_post.reshape(1, width))
+    )(u, tok, hidden, norm_post)
 
 
 def down_kernel(seg_ref, gate_ref, g_ref, w_ref, u_ref):

time: 256 us -> 249 us (0.973)
  local copies, waits for them, and re-layouts: 5.57 us -> 2.26 us
  Pallas kernels: 249 us -> 246 us
    pallas_call x1, Pallas kernels: 52.8 us -> 50.1 us  [finish(): pl.pallas_call(functools.partial(finish_kernel, ffn_size, emb_size, width...]
where the time goes in v4:
time: 249 us; the launch traced here: 248 us
  Pallas kernels  246 us (99%)
    pallas_call x1, Pallas kernels, exchange(): pl.pallas_call(functools.partial(exchange_kernel, emb_size, subs), out_sh...  121 us
    pallas_call x1, Pallas kernels, finish(): pl.pallas_call(functools.partial(finish_kernel, ffn_size, emb_size, width...  50.1 us
    pallas_call x1, Pallas kernels, dispatch_up(): pl.pallas_call(functools.partial(dispatch_up_kernel, steps), out_shape=ja...  41 us
    pallas_call x1, Pallas kernels, expert_down(): pl.pallas_call(down_kernel, out_shape=jax.ShapeDtypeStruct((rows, width),...  20.7 us
    pallas_call x1, Pallas kernels, prepare(): pl.pallas_call(functools.partial(prepare_kernel, capacity, emb_size, widt...  13.1 us

profile of v4, /device:TPU:97, one launch (start us, length us, event | category | flops | bytes accessed | tf_op | source)
XLA Modules:
  0.0 248.1 jit_solution(13772903479720689159)
XLA Ops:
  0.0 13.1 %prepare.1 = (s32[128,128]{1,0:T(8,128)}, s32[2,128]{1,0:T(2,128)}, f32[8,2048]{1,0:T(8,128)}, bf16[2048,256]{1,0:T(8,128)(2,1)}, f32[64,2048]{1,0:T(8,128)}) custom-call(s32[8,2048]{1,0:T(8,128)} %bitcast.2, bf16[2048,256]{1,0:T(8,128)(2,1)} %hid_ref.3, bf16[256]{0:T(256)(128)(2,1)} %pre_ref.1, bf16[64,256]{1,0:T(8,128)(2,1)} %bitcast.4), custom_call_target="tpu_custom_call" | custom-call | flops 15000000512 | bytes 4000000 | tf_op jit(solution)/shard_map/prepare/pallas_call | solution.py:149
  13.1 41.0 %dispatch_up.1.z_ref = bf16[16656,512]{1,0:T(8,128)(2,1)} custom-call(s32[2,128]{1,0:T(2,128)} %get-tuple-element.12.seg_ref, s32[128,128]{1,0:T(8,128)} %get-tuple-element.13.tok_ref, bf16[2048,256]{1,0:T(8,128)(2,1)} %get-tuple-element.14.b_ref, bf16[64,256,256]{2,1,0:T(8,128)(2,1)} %wg_ref.1, bf16[64,256,256]{2,1,0:T(8,128)(2,1)} %wu_ref.1), custom_call_target="tpu_custom_call" | custom-call | flops 21474836480 | bytes 33554432 | tf_op jit(solution)/shard_map/dispatch_up/pallas_call | solution.py:235
  54.1 120.9 %exchange.1 = (bf16[16656,256]{1,0:T(8,128)(2,1)}, f32[128,128]{1,0:T(8,128)}) custom-call(bf16[16656,512]{1,0:T(8,128)(2,1)} %dispatch_up.1.z_ref, f32[64,2048]{1,0:T(8,128)} %get-tuple-element.15.logit_ref, s32[8,2048]{1,0:T(8,128)} %bitcast.3, f32[8,2048]{1,0:T(8,128)} %get-tuple-element.16.pos_ref), custom_call_target="tpu_custom_call" | custom-call | flops 99999997952 | bytes 33554432 | tf_op jit(solution)/shard_map/exchange/pallas_call | solution.py:427
  175.0 20.7 %expert_down.1.u_ref = bf16[16656,256]{1,0:T(8,128)(2,1)} custom-call(s32[2,128]{1,0:T(2,128)} %get-tuple-element.12.seg_ref, f32[128,128]{1,0:T(8,128)} %get-tuple-element.17.gate_ref, bf16[16656,256]{1,0:T(8,128)(2,1)} %get-tuple-element.18.g_ref, bf16[64,256,256]{2,1,0:T(8,128)(2,1)} %w_ref.1), custom_call_target="tpu_custom_call" | custom-call | flops 2183135232 | bytes 17055744 | tf_op jit(solution)/shard_map/expert_down/pallas_call | solution.py:619
  195.8 50.1 %finish.1 = bf16[2048,256]{1,0:T(8,128)(2,1)} custom-call(bf16[16656,256]{1,0:T(8,128)(2,1)} %expert_down.1.u_ref, s32[128,128]{1,0:T(8,128)} %get-tuple-element.13.tok_ref, bf16[2048,256]{1,0:T(8,128)(2,1)} %hid_ref.3, bf16[256]{0:T(256)(128)(2,1)} %post_ref.1), custom_call_target="tpu_custom_call" | custom-call | flops 17179869184 | bytes 16000000 | tf_op jit(solution)/shard_map/finish/pallas_call | solution.py:575
  245.9 2.3 copy.10
